TPU v7x, 128 devices: a whole 4x4x4 slice. The times are simulated.
128 devices in a mesh: dp: 8 (over z, y_lo), tensor: 16 (over x, y_hi, core).
Axes of the slice: x: 4, y: 4 (y_hi: 2, y_lo: 2; y = y_hi * 2 + y_lo), z: 4, core: 2. Of those that a mesh axis runs over, the one named last changes fastest.
Arguments:
- projected: bfloat16 [2, 16384, 4608], P(None, ('dp', 'tensor')), may hold values from -60 to 60
- out_grad: bfloat16 [2, 16384, 4608], P(None, ('dp', 'tensor')), may hold values from -20 to 20
- attention: bfloat16 [2, 16384, 4096], P(None, 'dp', 'tensor'), may hold values from -6 to 6
- w_out: bfloat16 [4096, 4608], P('tensor'), may hold values from -0.09375 to 0.09375
- gains: float32 [4608], replicated, may hold values from 0.5 to 1.5
- main_out: float32 [4096, 4608], P('tensor', 'dp'), may hold values from -6 to 6
- main_gains: float32 [4608], replicated, may hold values from -6 to 6
Outputs:
- attn_grad: bfloat16 [2, 16384, 4096], P(None, 'dp', 'tensor')
- new_main_out: float32 [4096, 4608], P('tensor', 'dp')
- new_main_gains: float32 [4608], replicated
All inputs are finite; a program needn't handle non-finite values.
Results may differ from a plain program's by a relative error of at most 0.0049.
Values may be sent and summed in bfloat16 or wider, within the bound.
No kernel may reach another device: no remote copies, remote signals or barrier semaphores. Data moves between devices by JAX's collectives and lax.ppermute only.
A program may use at most 128 MiB of HBM per device.

v0:
```python
import functools
import math

import jax
import jax.numpy as jnp
from jax import lax
from jax.sharding import Mesh
from jax.sharding import PartitionSpec as P

DP = ("dp_0", "dp_1")
TENSOR = ("tensor_0", "tensor_1", "tensor_2")
DP_TENSOR = ("dp_0", "dp_1", "tensor_0", "tensor_1", "tensor_2")


def by_axis(value, axes):
    return functools.reduce(lax.psum, axes, value)


def cut_along(value, dim, size):
    before, after = (value.shape[:dim], value.shape[dim + 1 :])
    return jnp.moveaxis(value.reshape(*before, size, -1, *after), dim, 0)


def sent_and_summed(value, axis, dim):
    size = lax.axis_size(axis)
    parts = lax.all_to_all(cut_along(value, dim, size), axis, 0, 0, tiled=True)
    return jnp.sum(parts.astype(jnp.float32), axis=0)


def normalized(values):
    inverse = lax.rsqrt(jnp.mean(values * values, axis=-1, keepdims=True) + 1e-06)
    return (values * inverse, inverse)


def norm_back(upstream, normed, inverse):
    return inverse * (upstream - normed * jnp.mean(upstream * normed, axis=-1, keepdims=True))


def per_device(projected, out_grad, attention, w_out, gains, main_out, main_gains):
    micro_count = projected.shape[0]
    own_rows = projected.shape[1]
    tokens_all = micro_count * own_rows * lax.axis_size(DP) * lax.axis_size(TENSOR)
    factor = 1.0 / math.sqrt(tokens_all)
    gain_total = jnp.zeros(gains.shape, jnp.float32)
    back_list = []
    for micro_step in range(micro_count):
        output_in = projected[micro_step].astype(jnp.float32)
        upstream = out_grad[micro_step].astype(jnp.float32)
        out_hat, out_inv = normalized(output_in)
        out_gain = jnp.sum(upstream * out_hat, axis=0)
        out_back = norm_back(upstream * gains, out_hat, out_inv).astype(jnp.bfloat16)
        back_list.append(out_back)
        gain_total = gain_total + by_axis(out_gain, DP_TENSOR)
    stacked = jnp.stack(back_list)
    section = lax.all_gather(stacked, TENSOR, axis=1, tiled=True)
    weight_sum = lax.dot_general(
        attention, section, (((0, 1), (0, 1)), ((), ())), preferred_element_type=jnp.float32
    )
    product = lax.dot_general(
        section, w_out, (((2,), (1,)), ((), ())), preferred_element_type=jnp.float32
    ).astype(jnp.bfloat16)
    shard_out = sent_and_summed(weight_sum.astype(jnp.bfloat16), DP, 1)
    return (product, main_out + factor * shard_out, main_gains + factor * gain_total)


def solution(mesh):
    torus = Mesh(
        mesh.devices.reshape(4, 2, 4, 2, 2), ("dp_0", "dp_1", "tensor_0", "tensor_1", "tensor_2")
    )
    return jax.shard_map(
        per_device,
        mesh=torus,
        in_specs=(
            P(None, DP_TENSOR, None),
            P(None, DP_TENSOR, None),
            P(None, DP, TENSOR),
            P(TENSOR, None),
            P(),
            P(TENSOR, DP),
            P(),
        ),
        out_specs=(P(None, DP, TENSOR), P(TENSOR, DP), P()),
        check_vma=False,
    )
```

profile of v0, /device:TPU:1, one launch (start us, length us, event | category | flops | bytes accessed | tf_op | source)
XLA Modules:
  0.0 289.6 jit_solution(4183304599025154800)
XLA Ops:
  7.2 0.0 copy-start
  7.2 0.0 all-gather.2.cloned.1.call-start
  7.2 0.0 copy-start.1
  7.2 2.3 fusion.21
  9.6 0.2 copy-done.1
  9.8 0.0 copy-start.2
  9.8 0.0 copy-start.4
  9.8 3.5 %fusion.12 = (f32[128]{0:T(128)S(1)}, f32[128]{0:T(128)S(1)}, f32[4608]{0:T(1024)S(1)}, f32[4608]{0:T(1024)S(1)}) fusion(f32[128]{0:T(128)S(1)} %get-tuple-element.12, f32[4608]{0:T(1024)} %param.11, bf16[2,128,4608]{2,1,0:T(8,128)(2,1)} %param.8, bf16[2,128,4608]{2,1,0:T(8,128)(2,1)S(1)} %copy-done.1, f32[128]{0:T(128)S(1)} %get-tuple-element.11), kind=kLoop, calls=%fused_computation.23 | loop fusion | flops 9427712 | bytes 4775936 | tf_op jit(solution)/shard_map/reduce_sum | solution.py:36
  13.2 0.0 copy-done.2
  13.2 0.0 copy-done.4
  13.3 1.4 fusion.16
  14.7 1.6 pad_maximum_fusion
  16.3 0.0 copy-start.5
  16.3 0.0 all-gather.2.cloned.1.call-update
  16.3 15.3 %psum.84 = f32[4608]{0:T(1024)S(1)} all-reduce(f32[4608]{0:T(1024)S(1)} %add.48), channel_id=1, replica_groups=mesh['dp_0'=4,'dp_1'=2,'tensor_0'=4,'tensor_1'=2,'tensor_2'=2] {'dp_0'}, use_global_device_ids=true, to_apply=%region_6.0 | all-reduce | flops 4608 | bytes 36864 | tf_op jit(solution)/shard_map/psum | solution.py:16
  31.7 7.9 %psum.83 = f32[4608]{0:T(1024)S(1)} all-reduce(f32[4608]{0:T(1024)S(1)} %psum.84), channel_id=1, replica_groups=mesh['dp_0'=4,'dp_1'=2,'tensor_0'=4,'tensor_1'=2,'tensor_2'=2] {'dp_1'}, use_global_device_ids=true, to_apply=%region_7.0 | all-reduce | flops 4608 | bytes 36864 | tf_op jit(solution)/shard_map/psum | solution.py:16
  39.6 16.0 %psum.82 = f32[4608]{0:T(1024)S(1)} all-reduce(f32[4608]{0:T(1024)S(1)} %psum.83), channel_id=1, replica_groups=mesh['dp_0'=4,'dp_1'=2,'tensor_0'=4,'tensor_1'=2,'tensor_2'=2] {'tensor_0'}, use_global_device_ids=true, to_apply=%region_8.0 | all-reduce | flops 4608 | bytes 36864 | tf_op jit(solution)/shard_map/psum | solution.py:16
  55.5 9.5 %psum.81 = f32[4608]{0:T(1024)S(1)} all-reduce(f32[4608]{0:T(1024)S(1)} %psum.82), channel_id=1, replica_groups=mesh['dp_0'=4,'dp_1'=2,'tensor_0'=4,'tensor_1'=2,'tensor_2'=2] {'tensor_1'}, use_global_device_ids=true, to_apply=%region_9.0 | all-reduce | flops 4608 | bytes 36864 | tf_op jit(solution)/shard_map/psum | solution.py:16
  65.1 12.5 %psum.80 = f32[4608]{0:T(1024)S(1)} all-reduce(f32[4608]{0:T(1024)S(1)} %psum.81), channel_id=1, replica_groups=mesh['dp_0'=4,'dp_1'=2,'tensor_0'=4,'tensor_1'=2,'tensor_2'=2] {'tensor_2'}, use_global_device_ids=true, to_apply=%region_10.0 | all-reduce | flops 4608 | bytes 36864 | tf_op jit(solution)/shard_map/psum | solution.py:16
  77.5 0.0 copy-done.5
  77.5 0.6 multiply_add_fusion.1
  78.2 149.1 %all-gather.2.cloned.1.call-done = bf16[2,2048,4608]{2,1,0:T(8,128)(2,1)} async-done(((bf16[2,128,4608]{2,1,0:T(8,128)(2,1)}), bf16[2,2048,4608]{2,1,0:T(8,128)(2,1)}) %all-gather.2.cloned.1.call-update) | async-done | bytes 37748752 | tf_op jit(solution)/shard_map/all_gather | solution.py:55
  227.2 18.6 %fusion = bf16[4608,256]{1,0:T(8,128)(2,1)} fusion(bf16[2,2048,4608]{2,1,0:T(8,128)(2,1)} %all-gather.2.cloned.1.call-done, bf16[2,2048,256]{2,1,0:T(8,128)(2,1)} %param.9), kind=kOutput, calls=%fused_computation.1 | convolution fusion | flops 9664856064 | bytes 42205184 | tf_op jit(solution)/shard_map/dot_general | solution.py:56
  245.9 4.6 %all-to-all-start = ((bf16[8,256,576]{1,2,0:T(8,128)(2,1)}), bf16[8,256,576]{1,2,0:T(8,128)(2,1)}, u32[]{:S(2)}, u32[]{:S(2)}) async-start(bf16[8,256,576]{1,2,0:T(8,128)(2,1)} %bitcast.67), calls=%async_computation | async-start | bytes 4718592 | tf_op jit(solution)/shard_map/all_to_all | solution.py:26
  250.4 0.0 copy-done
  250.5 17.8 %convolution_convert_fusion = bf16[2,2048,256]{2,1,0:T(8,128)(2,1)} fusion(bf16[2,2048,4608]{2,1,0:T(8,128)(2,1)} %all-gather.2.cloned.1.call-done, bf16[256,4608]{1,0:T(8,128)(2,1)S(1)} %copy-done), kind=kOutput, calls=%fused_computation.3 | convolution fusion | flops 9664724992 | bytes 42205184 | tf_op jit(solution)/shard_map/dot_general | solution.py:59
  268.2 0.0 copy-start.3
  268.2 11.5 %all-to-all-done = bf16[8,256,576]{1,2,0:T(8,128)(2,1)} async-done(((bf16[8,256,576]{1,2,0:T(8,128)(2,1)}), bf16[8,256,576]{1,2,0:T(8,128)(2,1)}, u32[]{:S(2)}, u32[]{:S(2)}) %all-to-all-start) | async-done | bytes 2359328 | tf_op jit(solution)/shard_map/all_to_all | solution.py:26
  279.8 2.0 convert_reduce_fusion
  281.8 0.0 copy-done.3
  281.8 0.9 multiply_add_fusion
  (4 shorter events, 0.0 us)
Async XLA Ops:
  7.2 243.3 %copy-start = (bf16[256,4608]{1,0:T(8,128)(2,1)S(1)}, bf16[256,4608]{1,0:T(8,128)(2,1)}, u32[]{:S(2)}) copy-start(bf16[256,4608]{1,0:T(8,128)(2,1)} %param.10) | copy-start | bytes 7077892
  7.2 220.1 %all-gather.2.cloned.1.call-start = ((), (), s32[]{:S(2)}) async-start(), calls=%async_computation.1 | async-start | bytes 40108032 | tf_op jit(solution)/shard_map/all_gather | solution.py:55
  7.2 2.5 copy-start.1
  9.8 3.5 %copy-start.2 = (bf16[2,128,4608]{2,1,0:T(8,128)(2,1)S(1)}, bf16[2,128,4608]{2,1,0:T(8,128)(2,1)}, u32[]{:S(2)}) copy-start(bf16[2,128,4608]{2,1,0:T(8,128)(2,1)} %param.8) | copy-start | bytes 7077892
  9.8 3.5 %copy-start.4 = (f32[4608]{0:T(1024)S(1)}, f32[4608]{0:T(1024)}, u32[]{:S(2)}) copy-start(f32[4608]{0:T(1024)} %param.11) | copy-start | bytes 55300
  16.3 61.2 %copy-start.5 = (f32[4608]{0:T(1024)S(1)}, f32[4608]{0:T(1024)}, u32[]{:S(2)}) copy-start(f32[4608]{0:T(1024)} %param.13) | copy-start | bytes 55300
  245.9 33.9 %all-to-all-start = ((bf16[8,256,576]{1,2,0:T(8,128)(2,1)}), bf16[8,256,576]{1,2,0:T(8,128)(2,1)}, u32[]{:S(2)}, u32[]{:S(2)}) async-start(bf16[8,256,576]{1,2,0:T(8,128)(2,1)} %bitcast.67), calls=%async_computation | async-start | bytes 4718592 | tf_op jit(solution)/shard_map/all_to_all | solution.py:26
  268.2 13.6 %copy-start.3 = (f32[256,576]{0,1:T(8,128)S(1)}, f32[256,576]{0,1:T(8,128)}, u32[]{:S(2)}) copy-start(f32[256,576]{0,1:T(8,128)} %param.12) | copy-start | bytes 1769476
Sparse Core Ops, SparseCore 0:
  16.5 210.7 all-gather.1
where the time goes:
time: 290 us
  waiting for transfers between devices  161 us (56%)
  blocking collectives  61.2 us (21%)
  matrix products  36.4 us (13%)
  between operations  14.1 us (5%)
  other arithmetic  12.4 us (4%)
  starting transfers between devices  4.6 us (2%)
    all_gather x1, waiting for transfers between devices, per_device(): section = lax.all_gather(stacked, TENSOR, axis=1, tiled=True)  149 us
    psum x5, blocking collectives, by_axis(): return functools.reduce(lax.psum, axes, value)  61.2 us
    dot_general x1, matrix products, per_device(): lax.dot_general(attention, section, (((0, 1), (0, 1)), ((), ())), preferr...  18.6 us
    dot_general x1, matrix products, per_device(): lax.dot_general(section, w_out, (((2,), (1,)), ((), ())), preferred_eleme...  17.8 us
    all_to_all x1, waiting for transfers between devices, sent_and_summed(): parts = lax.all_to_all(cut_along(value, dim, size), axis, 0, 0, tiled=True)  11.5 us
  transfers between devices with their start and end apart: 2, of which 2 were waited for; matrix products, arithmetic and copies ran while one was open for 6% of the time, Pallas kernels for 0%

commit v1 on v0

v1 whole, which is shorter than its diff:
```python
import functools
import math

import jax
import jax.numpy as jnp
from jax import lax
from jax.experimental import pallas as pl
from jax.experimental.pallas import tpu as pltpu
from jax.sharding import Mesh
from jax.sharding import PartitionSpec as P

Z, YL, X, YH, C = AXES = ("dp_0", "dp_1", "tensor_0", "tensor_1", "tensor_2")
DP = (Z, YL)
TENSOR = (X, YH, C)
BF16 = jnp.bfloat16
F32 = jnp.float32

PIECES = (((0, 512),), ((512, 384),), ((896, 256),))
SIZES = tuple(sum(size for _, size in runs) for runs in PIECES)
SUMS = ((0,), (1, 2))
RELATIVE = (0, -1, 1, 2)


def ring(step, size=4):
    return [(i, (i + step) % size) for i in range(size)]


def swap(size=2):
    return [(i, size - 1 - i) for i in range(size)]


def params(semantics, mib=56):
    return pltpu.CompilerParams(dimension_semantics=semantics, vmem_limit_bytes=mib * 1024 * 1024)


def cost(flops, moved):
    return pl.CostEstimate(flops=flops, bytes_accessed=moved, transcendentals=0)


def nt(lhs, rhs):
    return lax.dot_general(lhs, rhs, (((1,), (1,)), ((), ())), preferred_element_type=F32)


def near(position, j):
    if not isinstance(j, int):
        offset = jnp.where(j == 1, 3, jnp.where(j == 2, 1, jnp.where(j == 3, 2, 0)))
    else:
        offset = RELATIVE[j] % 4
    return lax.rem(position + offset, 4)


def norm_kernel(width, values, upstream, gains, *outs):
    pieces, total = outs[:-1], outs[-1]
    v = values[0].astype(F32)
    u = upstream[0].astype(F32)
    inverse = lax.rsqrt(jnp.mean(v * v, axis=-1, keepdims=True) + 1e-06)
    n = v * inverse
    gain = jnp.sum((u * n).reshape(-1, 8, u.shape[-1]), axis=0)

    @pl.when((pl.program_id(0) == 0) & (pl.program_id(1) == 0))
    def _():
        total[...] = jnp.zeros_like(total)

    total[...] += gain
    w = u * gains[...][None, :]
    back = (inverse * (w - n * jnp.mean(w * n, axis=-1, keepdims=True))).astype(BF16)
    for runs, out in zip(PIECES, pieces):
        at = 0
        for z in range(4):
            for start, size in runs:
                out[0, :, at : at + size] = back[:, z * width + start : z * width + start + size]
                at += size


def norm_pieces(projected, out_grad, gains, step=64):
    micro, rows, cols = projected.shape
    block = pl.BlockSpec((1, step, cols), lambda m, i: (m, i, 0))
    return pl.pallas_call(
        functools.partial(norm_kernel, cols // 4),
        grid=(micro, rows // step),
        in_specs=[block, block, pl.BlockSpec((cols,), lambda m, i: (0,))],
        out_specs=[pl.BlockSpec((1, step, 4 * s), lambda m, i: (m, i, 0)) for s in SIZES]
        + [pl.BlockSpec((8, cols), lambda m, i: (0, 0))],
        out_shape=[jax.ShapeDtypeStruct((micro, rows, 4 * s), BF16) for s in SIZES]
        + [jax.ShapeDtypeStruct((8, cols), F32)],
        compiler_params=params(("arbitrary", "arbitrary")),
        cost_estimate=cost(16 * micro * rows * cols, 6 * micro * rows * cols),
        name="norm_back",
    )(projected, out_grad, gains)


def turn_kernel(place, eye, *refs):
    mine, over = refs[-2:]
    rows = jnp.concatenate([r[0, 0] for r in refs[:-2]], axis=0)
    part = nt(eye[...], rows).astype(BF16)

    @pl.when(pl.program_id(0) < 2)
    def _():
        over[0] = part

    @pl.when(pl.program_id(0) >= 2)
    def _():
        mine[0] = part


def turned(attention, place):
    micro, rows, heads = attention.shape
    each = rows // 16
    blocks = attention.reshape(micro, 16, each, heads)

    def spec(j, m):
        def index(i, p):
            return (m, near(p[0], j) * 4 + (p[1] ^ 1 ^ (i // 2)) * 2 + (p[2] ^ (i % 2)), 0, 0)

        return pl.BlockSpec((1, 1, each, heads), index)

    specs = [spec(j, m) for j in range(4) for m in range(micro)]
    shape = (2, heads, 4 * micro * each)
    block = (1,) + shape[1:]
    return pl.pallas_call(
        turn_kernel,
        grid_spec=pltpu.PrefetchScalarGridSpec(
            num_scalar_prefetch=1,
            grid=(4,),
            in_specs=[pl.BlockSpec((heads, heads), lambda i, p: (0, 0))] + specs,
            out_specs=[
                pl.BlockSpec(block, lambda i, p: (jnp.maximum(i - 2, 0), 0, 0)),
                pl.BlockSpec(block, lambda i, p: (jnp.minimum(i, 1), 0, 0)),
            ],
        ),
        out_shape=[jax.ShapeDtypeStruct(shape, BF16)] * 2,
        compiler_params=params(("arbitrary",)),
        cost_estimate=cost(8 * heads * heads * shape[2], 16 * heads * shape[2]),
        name="turn",
    )(place, jnp.eye(heads, dtype=BF16), *([blocks] * len(specs)))


def data_kernel(plan, carried, last, place, *refs):
    del place
    acc, refs = refs[-1], list(refs[:-1])
    step = pl.program_id(0)
    sides = []
    for pieces, number in plan:
        parts = []
        for _ in pieces:
            take, refs = refs[:number], refs[number:]
            parts.append(jnp.concatenate([r[...].reshape(-1, r.shape[-1]) for r in take], axis=0))
        sides.append(parts[0] if len(parts) == 1 else jnp.concatenate(parts, axis=1))
    weights, refs = refs[:4], refs[4:]
    before = refs.pop(0) if carried else None

    @pl.when(step == 0)
    def _():
        acc[...] = jnp.zeros_like(acc)
        if carried:
            acc[:, : before.shape[1]] = before[...]

    for h, w in enumerate(weights):
        at = 0
        for (pieces, _), lhs in zip(plan, sides):
            start = PIECES[pieces[0]][0][0]
            columns = slice(start, start + lhs.shape[1])
            acc[h, at : at + lhs.shape[0]] += nt(lhs, w[:, columns])
            at += lhs.shape[0]

    @pl.when(step == 3)
    def _():
        for h in range(4):
            if last:
                out = refs[h // 2]
                out[h % 2] = acc[h].astype(BF16).reshape(out.shape[1:])
            else:
                refs[0][h] = acc[h]


def data_grad(place, plan, weights, before=None, last=True):
    flat = [a for _, arrays in plan for piece in arrays for a in piece]
    width = weights[0].shape[1] // 4
    rows = sum(sum(math.prod(a.shape[:-1]) for a in arrays[0]) for _, arrays in plan)

    def rows_spec(a):
        size = a.shape[-1] // 4
        if len(a.shape) == 3:
            return pl.BlockSpec(a.shape[:2] + (size,), lambda t, p: (0, 0, t))
        return pl.BlockSpec((a.shape[0], size), lambda t, p: (0, t))

    held = pl.BlockSpec((4, rows if before is None else before.shape[1], 256), lambda t, p: (0, 0, 0))
    shape = (2, rows // 256, 2, 128, 256)
    args = [*flat, *weights]
    specs = [rows_spec(a) for a in flat] + [pl.BlockSpec((256, width), lambda t, p: (0, t))] * 4
    if before is not None:
        args.append(before)
        specs.append(held)
    flops = sum(
        2 * math.prod(a.shape) * 1024 for _, arrays in plan for piece in arrays for a in piece
    )
    return pl.pallas_call(
        functools.partial(
            data_kernel, [(k, len(a[0])) for k, a in plan], before is not None, last
        ),
        grid_spec=pltpu.PrefetchScalarGridSpec(
            num_scalar_prefetch=1,
            grid=(4,),
            in_specs=specs,
            out_specs=[pl.BlockSpec(shape, lambda t, p: (0, 0, 0, 0, 0))] * 2 if last else held,
            scratch_shapes=[pltpu.VMEM((4, rows, 256), F32)],
        ),
        out_shape=[jax.ShapeDtypeStruct(shape, BF16)] * 2
        if last
        else jax.ShapeDtypeStruct((4, rows, 256), F32),
        compiler_params=params(("arbitrary",)),
        cost_estimate=cost(flops, 8 * 1024 * width),
        name="data_grad",
    )(place, *args)


def weight_sum(pieces, heads):
    sizes = [piece[0].shape[2] // 4 for piece in pieces]
    total = sum(sizes)
    zs = 1 if total % 512 == 0 else 2
    out = pl.BlockSpec((zs, 2, 256, total), lambda i: (i, 0, 0, 0))
    one = pl.BlockSpec((1, 256, 1024), lambda i: (0, 0, 0))
    two = pl.BlockSpec((2, 256, 1024), lambda i: (0, 0, 0))
    specs = []
    for size in sizes:
        specs += [pl.BlockSpec((2, 128, zs * size), lambda i: (0, 0, i))] * 3
        specs += [pl.BlockSpec((128, zs * size), lambda i: (0, i))] * 2
    mine, over, mates = heads

    def kernel(*refs):
        mine, over, mates, keep, send = refs[-5:]
        at = 0
        for k, size in enumerate(sizes):
            rows = jnp.concatenate(
                [r[...].reshape(-1, zs * size) for r in refs[5 * k : 5 * k + 5]], axis=0
            )
            for to, h, block in (
                (keep, 0, mine[0]),
                (keep, 1, over[0]),
                (send, 0, mates[0]),
                (send, 1, mates[1]),
            ):
                part = jnp.dot(block, rows, preferred_element_type=F32).astype(BF16)
                for n in range(zs):
                    to[n, h, :, at : at + size] = part[:, n * size : (n + 1) * size]
            at += size

    return pl.pallas_call(
        kernel,
        grid=(4 // zs,),
        in_specs=specs + [one, one, two],
        out_specs=[out] * 2,
        out_shape=[jax.ShapeDtypeStruct((4, 2, 256, total), BF16)] * 2,
        compiler_params=params(("arbitrary",)),
        cost_estimate=cost(8 * 1024 * 1024 * total, 20 * 1024 * total),
        name="weight_sum",
    )(*[a for piece in pieces for a in piece], mine, over, mates)


def place_kernel(place, mine, over, mates, out):
    for j in range(4):
        for h, block in enumerate((mine.at[0], mates.at[0], over.at[0], mates.at[1])):
            at = near(place[0], j) * 4 + (place[1] ^ (h // 2)) * 2 + (place[2] ^ (h % 2))
            out[:, pl.ds(at, 1)] = block[j][:, None]


def placed(place, blocks):
    mine, over, mates = blocks
    shape = mine.shape[1:]
    one = pl.BlockSpec((1,) + shape, lambda i, p: (0, 0, 0, 0, 0))
    two = pl.BlockSpec((2,) + shape, lambda i, p: (0, 0, 0, 0, 0))
    return pl.pallas_call(
        place_kernel,
        grid_spec=pltpu.PrefetchScalarGridSpec(
            num_scalar_prefetch=1,
            grid=(1,),
            in_specs=[one, one, two],
            out_specs=pl.BlockSpec((2, 16, 128, 256), lambda i, p: (0, 0, 0, 0)),
        ),
        out_shape=jax.ShapeDtypeStruct((2, 16, 128, 256), BF16),
        compiler_params=params(("arbitrary",)),
        cost_estimate=cost(1000000, 16 * 1024 * 1024 // 2),
        name="place",
    )(place, mine, over, mates)


def moved(value, axis, pairs):
    return lax.ppermute(value, axis, pairs)


def per_device(projected, out_grad, attention, w_out, gains, main_out, main_gains):
    micro, own_rows, cols = projected.shape
    tokens_all = micro * own_rows * lax.axis_size(AXES)
    factor = 1.0 / math.sqrt(tokens_all)
    here, low = lax.axis_index(Z), lax.axis_index(YL)
    place = jnp.stack([lax.axis_index(X), lax.axis_index(YH), lax.axis_index(C)])

    *own, gain = norm_pieces(projected, out_grad, gains)
    left = [moved(p, X, ring(1)) for p in own]
    right = [moved(p, X, ring(-1)) for p in own]
    far = []
    for k in range(len(own)):
        a, b = left[k][0], right[k][1]
        far.append((moved(a, X, ring(1)), moved(b, X, ring(-1))))

    def exchanged(mine, over):
        over = moved(over, YH, swap())
        mates = jnp.stack([mine[1], over[1]])
        return mine, over, moved(mates, C, swap())

    heads = exchanged(*turned(attention, place))

    over = moved(w_out, (YL, YH), swap(4))
    weights = (w_out, moved(w_out, C, swap()), over, moved(over, C, swap()))

    gain = jnp.sum(gain, axis=0)
    for axis, bit in ((YH, 1), (YL, 1), (Z, 1), (Z, 2), (C, 1), (X, 1), (X, 2)):
        pairs = [(i, i ^ bit) for i in range(lax.axis_size(axis))]
        gain = gain + moved(gain, axis, pairs)
    new_gains = main_gains + factor * gain

    plan = [
        (tuple(range(len(own))), [(own[k], left[k], right[k]) for k in range(len(own))]),
        (tuple(range(len(own))), far),
    ]
    outs = data_grad(place, plan, weights)
    grad = placed(place, exchanged(*outs))

    def reduced(k):
        pieces = [(own[i], left[i], right[i], *far[i]) for i in SUMS[k]]
        keep, send = weight_sum(pieces, heads)
        other = moved(send, C, swap())

        def block(step):
            at = lax.rem(here + step + 4, 4)
            a = lax.dynamic_index_in_dim(keep, at, 0, keepdims=False).astype(F32)
            return a + lax.dynamic_index_in_dim(other, at, 0, keepdims=False).astype(F32)

        got = [moved(block(step).astype(BF16), Z, ring(step)) for step in (1, -1, 2)]
        return (block(0) + sum(g.astype(F32) for g in got)).astype(BF16)

    whole = jnp.concatenate([reduced(k) for k in range(len(SUMS))], axis=2)
    first, second = whole[:, :, : cols // 8], whole[:, :, cols // 8 :]
    ours, theirs = jnp.where(low == 0, first, second), jnp.where(low == 0, second, first)
    total = ours[0].astype(F32)
    for value, axes, pairs in ((theirs[0], YL, swap()), (ours[1], YH, swap()), (theirs[1], (YL, YH), swap(4))):
        total += moved(value, axes, pairs).astype(F32)
    return (grad.reshape(attention.shape), main_out + factor * total, new_gains)


def solution(mesh):
    torus = Mesh(mesh.devices.reshape(4, 2, 4, 2, 2), AXES)

    return jax.shard_map(
        per_device,
        mesh=torus,
        in_specs=(
            P(None, AXES, None),
            P(None, AXES, None),
            P(None, DP, TENSOR),
            P(TENSOR, None),
            P(),
            P(TENSOR, DP),
            P(),
        ),
        out_specs=(P(None, DP, TENSOR), P(TENSOR, DP), P()),
        check_vma=False,
    )
```

time: 290 us -> 208 us (0.72)
  waiting for transfers between devices: 161 us -> 73.8 us
  blocking collectives: 61.2 us -> 0 us
  starting transfers between devices: 4.6 us -> 56.9 us
  Pallas kernels: 0 us -> 50.5 us
  matrix products: 36.4 us -> 0 us
  between operations: 14.1 us -> 0.96 us
  local copies, waits for them, and re-layouts: 0.2 us -> 10.6 us
    all_gather x1 -> x0, waiting for transfers between devices: 149 us -> none  [per_device(): section = lax.all_gather(stacked, TENSOR, axis=1, tiled=True)]
    ppermute x0 -> x37, waiting for transfers between devices: none -> 73.8 us  [moved(): return lax.ppermute(value, axis, pairs)]
    psum x5 -> x0, blocking collectives: 61.2 us -> none  [by_axis(): return functools.reduce(lax.psum, axes, value)]
    ppermute x0 -> x37, starting transfers between devices: none -> 56.9 us  [moved(): return lax.ppermute(value, axis, pairs)]
    pallas_call x0 -> x6, Pallas kernels: none -> 50.5 us  [the longest x2 17.7 us: weight_sum(): pl.pallas_call(kernel, grid=(4 // zs,), in_specs=specs + [one, one, two],...]
    dot_general x2 -> x0, matrix products: 36.4 us -> none  [the longest x1 18.6 us: per_device(): lax.dot_general(attention, section, (((0, 1), (0, 1)), ((), ())), preferr...]
    all_to_all x1 -> x0, waiting for transfers between devices: 11.5 us -> none  [sent_and_summed(): parts = lax.all_to_all(cut_along(value, dim, size), axis, 0, 0, tiled=True)]
    convert_element_type x1 -> x5, other arithmetic: 1.44 us -> 11.2 us  [the longest x2 6.42 us: reduced(): block(step).astype(BF16)]
  transfers between devices with their start and end apart: 2 -> 37, of which waited for: 2 -> 16; matrix products, arithmetic and copies ran while one was open for 6% -> 10% of each run, Pallas kernels for 0% -> 20%
where the time goes in v1:
time: 208 us; the launch traced here: 207 us
  waiting for transfers between devices  73.8 us (35%)
  starting transfers between devices  56.9 us (27%)
  Pallas kernels  50.5 us (24%)
  other arithmetic  14.5 us (7%)
  local copies, waits for them, and re-layouts  10.6 us (5%)
    ppermute x37, waiting for transfers between devices, moved(): return lax.ppermute(value, axis, pairs)  73.8 us
    ppermute x37, starting transfers between devices, moved(): return lax.ppermute(value, axis, pairs)  56.9 us
    pallas_call x2, Pallas kernels, weight_sum(): pl.pallas_call(kernel, grid=(4 // zs,), in_specs=specs + [one, one, two],...  17.7 us
    pallas_call x1, Pallas kernels, data_grad(): pl.pallas_call(functools.partial(data_kernel, [(k, len(a[0])) for k, a in...  17.4 us
    unnamed x44, local copies, waits for them, and re-layouts  6.57 us
    convert_element_type x2, other arithmetic, reduced(): block(step).astype(BF16)  6.42 us
    pallas_call x1, Pallas kernels, norm_pieces(): pl.pallas_call(functools.partial(norm_kernel, cols // 4), grid=(micro, ro...  5.95 us
    pallas_call x1, Pallas kernels, turned(): pl.pallas_call(turn_kernel, grid_spec=pltpu.PrefetchScalarGridSpec(num_sc...  5.69 us
  transfers between devices with their start and end apart: 37, of which 16 were waited for; matrix products, arithmetic and copies ran while one was open for 10% of the time, Pallas kernels for 20%

profile of v1, /device:TPU:1, one launch (start us, length us, event | category | flops | bytes accessed | tf_op | source)
XLA Modules:
  0.0 207.2 jit_solution(4684456198544323342)
XLA Ops:
  0.6 6.0 %norm_back.1 = (bf16[2,128,2048]{2,1,0:T(8,128)(2,1)}, bf16[2,128,1536]{2,1,0:T(8,128)(2,1)}, bf16[2,128,1024]{2,1,0:T(8,128)(2,1)}, f32[8,4608]{1,0:T(8,128)}) custom-call(bf16[2,128,4608]{2,1,0:T(8,128)(2,1)} %values.1, bf16[2,128,4608]{2,1,0:T(8,128)(2,1)} %upstream.1, f32[4608]{0:T(1024)} %gains.1), custom_call_target="tpu_custom_call" | custom-call | flops 18874368 | bytes 7077888 | tf_op jit(solution)/shard_map/norm_back/pallas_call | solution.py:78
  6.6 2.0 collective-permute-start.4
  11.4 5.7 %turn.1 = (bf16[2,256,1024]{2,1,0:T(8,128)(2,1)}, bf16[2,256,1024]{2,1,0:T(8,128)(2,1)}) custom-call(s32[3]{0:T(128)} %pad_add_fusion.place, bf16[256,256]{1,0:T(8,128)(2,1)} %fusion.12.eye, bf16[2,16,128,256]{3,2,1,0:T(8,128)(2,1)} %bitcast.48, bf16[2,16,128,256]{3,2,1,0:T(8,128)(2,1)} %bitcast.49, bf16[2,16,128,256]{3,2,1,0:T(8,128)(2,1)} %bitcast.50, ...), custom_call_target="tpu_custom_call" | custom-call | flops 536870912 | bytes 4194304 | tf_op jit(solution)/shard_map/turn/pallas_call | solution.py:120
  17.1 3.0 %collective-permute-start.17 = (bf16[2,256,1024]{2,1,0:T(8,128)(2,1)}, bf16[2,256,1024]{2,1,0:T(8,128)(2,1)S(1)}, u32[]{:S(2)}, u32[]{:S(2)}) collective-permute-start(bf16[2,256,1024]{2,1,0:T(8,128)(2,1)} %get-tuple-element.21), channel_id=1, source_target_pairs={{0,2},{2,0},{1,3},{3,1},{4,6},{6,4},{5,7},{7,5},{8,10},{10,8},{9,1... | collective-permute-start | bytes 3145736 | tf_op jit(solution)/shard_map/ppermute | solution.py:288
  25.5 12.7 %collective-permute-done.2.refs_4_.refs_1_ = bf16[2,128,1536]{2,1,0:T(8,128)(2,1)S(1)} collective-permute-done((bf16[2,128,1536]{2,1,0:T(8,128)(2,1)}, bf16[2,128,1536]{2,1,0:T(8,128)(2,1)S(1)}, u32[]{:S(2)}, u32[]{:S(2)}) %collective-permute-start.2) | collective-permute-done | bytes 786464 | tf_op jit(solution)/shard_map/ppermute | solution.py:288
  38.2 3.0 %collective-permute-start.13 = (bf16[256,4608]{1,0:T(8,128)(2,1)}, bf16[256,4608]{1,0:T(8,128)(2,1)}, u32[]{:S(2)}, u32[]{:S(2)}) collective-permute-start(bf16[256,4608]{1,0:T(8,128)(2,1)} %refs_15_.1), channel_id=1, source_target_pairs={{0,18},{2,16},{16,2},{18,0},{1,19},{3,17},{17,3},{19,1},{4,22},{6,... | collective-permute-start | bytes 7077896 | tf_op jit(solution)/shard_map/ppermute | solution.py:288
  43.4 18.8 %collective-permute-done.3.refs_5_.refs_2_ = bf16[2,128,1536]{2,1,0:T(8,128)(2,1)S(1)} collective-permute-done((bf16[2,128,1536]{2,1,0:T(8,128)(2,1)S(1)}, bf16[2,128,1536]{2,1,0:T(8,128)(2,1)S(1)}, u32[]{:S(2)}, u32[]{:S(2)}) %collective-permute-start.3) | collective-permute-done | bytes 786464 | tf_op jit(solution)/shard_map/ppermute | solution.py:288
  62.2 2.8 %collective-permute-start.18 = (bf16[2,256,1024]{2,1,0:T(8,128)(2,1)S(1)}, bf16[2,256,1024]{2,1,0:T(8,128)(2,1)S(1)}, u32[]{:S(2)}, u32[]{:S(2)}) collective-permute-start(bf16[2,256,1024]{2,1,0:T(8,128)(2,1)S(1)} %pad_maximum_fusion.1), channel_id=1, source_target_pairs={{0,1},{1,0},{2,3},{3,2},{4,5},{5,4},{6,7},{7,6},{8,9},{9,8},{10,11... | collective-permute-start | bytes 3145736 | tf_op jit(solution)/shard_map/ppermute | solution.py:288
  65.1 2.7 %collective-permute-start.11 = (bf16[128,1024]{1,0:T(8,128)(2,1)S(1)}, bf16[128,1024]{1,0:T(8,128)(2,1)S(1)}, u32[]{:S(2)}, u32[]{:S(2)}) collective-permute-start(bf16[128,1024]{1,0:T(8,128)(2,1)S(1)} %slice_bitcast_fusion.8), channel_id=1, source_target_pairs={{0,12},{4,0},{8,4},{12,8},{1,13},{5,1},{9,5},{13,9},{2,14},{6,2},{... | collective-permute-start | bytes 786440 | tf_op jit(solution)/shard_map/ppermute | solution.py:288
  68.6 2.1 %collective-permute-start.9 = (bf16[128,1536]{1,0:T(8,128)(2,1)S(1)}, bf16[128,1536]{1,0:T(8,128)(2,1)S(1)}, u32[]{:S(2)}, u32[]{:S(2)}) collective-permute-start(bf16[128,1536]{1,0:T(8,128)(2,1)S(1)} %slice_bitcast_fusion.2), channel_id=1, source_target_pairs={{0,12},{4,0},{8,4},{12,8},{1,13},{5,1},{9,5},{13,9},{2,14},{6,2},{... | collective-permute-start | bytes 1179656 | tf_op jit(solution)/shard_map/ppermute | solution.py:288
  70.8 2.7 %collective-permute-done.11.refs_14_.refs_9_ = bf16[128,1024]{1,0:T(8,128)(2,1)S(1)} collective-permute-done((bf16[128,1024]{1,0:T(8,128)(2,1)S(1)}, bf16[128,1024]{1,0:T(8,128)(2,1)S(1)}, u32[]{:S(2)}, u32[]{:S(2)}) %collective-permute-start.11) | collective-permute-done | bytes 262176 | tf_op jit(solution)/shard_map/ppermute | solution.py:288
  74.0 5.6 %collective-permute-done.8.refs_11_.refs_3_ = bf16[128,1536]{1,0:T(8,128)(2,1)S(1)} collective-permute-done((bf16[128,1536]{1,0:T(8,128)(2,1)S(1)}, bf16[128,1536]{1,0:T(8,128)(2,1)S(1)}, u32[]{:S(2)}, u32[]{:S(2)}) %collective-permute-start.8) | collective-permute-done | bytes 393248 | tf_op jit(solution)/shard_map/ppermute | solution.py:288
  79.7 2.2 %collective-permute-done.9.refs_12_.refs_4_ = bf16[128,1536]{1,0:T(8,128)(2,1)S(1)} collective-permute-done((bf16[128,1536]{1,0:T(8,128)(2,1)S(1)}, bf16[128,1536]{1,0:T(8,128)(2,1)S(1)}, u32[]{:S(2)}, u32[]{:S(2)}) %collective-permute-start.9) | collective-permute-done | bytes 393248 | tf_op jit(solution)/shard_map/ppermute | solution.py:288
  83.6 9.7 %weight_sum.3 = (bf16[4,2,256,640]{3,2,1,0:T(8,128)(2,1)}, bf16[4,2,256,640]{3,2,1,0:T(8,128)(2,1)}) custom-call(bf16[2,128,1536]{2,1,0:T(8,128)(2,1)} %get-tuple-element.16.refs_3_.refs_0_, bf16[2,128,1536]{2,1,0:T(8,128)(2,1)} %copy-done.7, bf16[2,128,1536]{2,1,0:T(8,128)(2,1)} %copy-done.8, bf16[128,1536]{1,0:T(8,128)(2,1)} %copy-done.17, ...), custom_call_target="tpu_custom_call" | custom-call | flops 5368709120 | bytes 13107200 | tf_op jit(solution)/shard_map/weight_sum/pallas_call | solution.py:248
  96.4 8.0 %weight_sum.2 = (bf16[4,2,256,512]{3,2,1,0:T(8,128)(2,1)}, bf16[4,2,256,512]{3,2,1,0:T(8,128)(2,1)}) custom-call(bf16[2,128,2048]{2,1,0:T(8,128)(2,1)} %get-tuple-element.15.refs_0_, bf16[2,128,2048]{2,1,0:T(8,128)(2,1)} %copy-done.4, bf16[2,128,2048]{2,1,0:T(8,128)(2,1)} %copy-done.5, bf16[128,2048]{1,0:T(8,128)(2,1)} %copy-done.15, ...), custom_call_target="tpu_custom_call" | custom-call | flops 4294967296 | bytes 10485760 | tf_op jit(solution)/shard_map/weight_sum/pallas_call | solution.py:248
  105.1 3.8 %collective-permute-done.19 = bf16[4,2,256,512]{3,2,1,0:T(8,128)(2,1)S(1)} collective-permute-done((bf16[4,2,256,512]{3,2,1,0:T(8,128)(2,1)}, bf16[4,2,256,512]{3,2,1,0:T(8,128)(2,1)S(1)}, u32[]{:S(2)}, u32[]{:S(2)}) %collective-permute-start.19) | collective-permute-done | bytes 2097184 | tf_op jit(solution)/shard_map/ppermute | solution.py:288
  110.1 3.4 %fusion.9 = (bf16[2,256,512]{2,1,0:T(8,128)(2,1)}, bf16[2,256,512]{2,1,0:T(8,128)(2,1)}, bf16[2,256,512]{2,1,0:T(8,128)(2,1)}) fusion(bf16[4,2,256,512]{3,2,1,0:T(8,128)(2,1)} %copy-done.2, s32[]{:T(128)S(6)} %select_n.40, bf16[4,2,256,512]{3,2,1,0:T(8,128)(2,1)} %get-tuple-element.22, s32[]{:T(128)S(6)} %select_n.42, s32[]{:T(128)S(6)} %select_n.41), kind=kLoop, calls=%fused_computation.23 | loop fusion | flops 3145728 | bytes 4718604 | tf_op jit(solution)/shard_map/convert_element_type | solution.py:339
  115.2 2.0 collective-permute-start.30
  117.3 2.2 %collective-permute-done.30 = f32[4608]{0:T(1024)S(1)} collective-permute-done((f32[4608]{0:T(1024)S(1)}, f32[4608]{0:T(1024)S(1)}, u32[]{:S(2)}, u32[]{:S(2)}) %collective-permute-start.30) | collective-permute-done | bytes 18464 | tf_op jit(solution)/shard_map/ppermute | solution.py:288
  120.2 2.2 %collective-permute-done.31 = f32[4608]{0:T(1024)S(1)} collective-permute-done((f32[4608]{0:T(1024)S(1)}, f32[4608]{0:T(1024)S(1)}, u32[]{:S(2)}, u32[]{:S(2)}) %collective-permute-start.31) | collective-permute-done | bytes 18464 | tf_op jit(solution)/shard_map/ppermute | solution.py:288
  126.1 3.0 %fusion.2 = (bf16[2,256,640]{2,1,0:T(8,128)(2,1)}, bf16[2,256,640]{2,1,0:T(8,128)(2,1)S(1)}, bf16[2,256,640]{2,1,0:T(8,128)(2,1)}) fusion(bf16[4,2,256,640]{3,2,1,0:T(8,128)(2,1)} %collective-permute-done.23, s32[]{:T(128)S(6)} %select_n.40, bf16[4,2,256,640]{3,2,1,0:T(8,128)(2,1)S(1)} %copy-done, s32[]{:T(128)S(6)} %select_n.42, s32[]{:T(128)S(6)} %select_n.41), kind=kLoop, calls=%fused_computation.12 | loop fusion | flops 3932160 | bytes 5898252 | tf_op jit(solution)/shard_map/convert_element_type | solution.py:339
  133.8 17.4 %data_grad.1 = (bf16[2,4,2,128,256]{4,3,2,1,0:T(8,128)(2,1)}, bf16[2,4,2,128,256]{4,3,2,1,0:T(8,128)(2,1)}) custom-call(s32[3]{0:T(128)} %pad_add_fusion.place, bf16[2,128,2048]{2,1,0:T(8,128)(2,1)} %get-tuple-element.15.refs_0_, bf16[2,128,2048]{2,1,0:T(8,128)(2,1)} %copy-done.4, bf16[2,128,2048]{2,1,0:T(8,128)(2,1)} %copy-done.5, ...), custom_call_target="tpu_custom_call" | custom-call | flops 9663676416 | bytes 9437184 | tf_op jit(solution)/shard_map/data_grad/pallas_call | solution.py:197
  151.3 2.1 collective-permute-start.15
  153.3 2.2 %collective-permute-start.33 = (f32[4608]{0:T(1024)S(1)}, f32[4608]{0:T(1024)S(1)}, u32[]{:S(2)}, u32[]{:S(2)}) collective-permute-start(f32[4608]{0:T(1024)S(1)} %add.174), channel_id=1, source_target_pairs={{0,64},{32,96},{64,0},{96,32},{1,65},{33,97},{65,1},{97,33},{2,66}... | collective-permute-start | bytes 55304 | tf_op jit(solution)/shard_map/ppermute | solution.py:288
  157.6 4.4 %collective-permute-done.24 = bf16[2,256,640]{2,1,0:T(8,128)(2,1)} collective-permute-done((bf16[2,256,640]{2,1,0:T(8,128)(2,1)}, bf16[2,256,640]{2,1,0:T(8,128)(2,1)}, u32[]{:S(2)}, u32[]{:S(2)}) %collective-permute-start.24) | collective-permute-done | bytes 655392 | tf_op jit(solution)/shard_map/ppermute | solution.py:288
  162.0 7.7 %collective-permute-done.26 = bf16[2,256,640]{2,1,0:T(8,128)(2,1)} collective-permute-done((bf16[2,256,640]{2,1,0:T(8,128)(2,1)S(1)}, bf16[2,256,640]{2,1,0:T(8,128)(2,1)}, u32[]{:S(2)}, u32[]{:S(2)}) %collective-permute-start.26) | collective-permute-done | bytes 655392 | tf_op jit(solution)/shard_map/ppermute | solution.py:288
  169.7 2.1 %fusion = bf16[2,256,640]{2,1,0:T(8,128)(2,1)S(1)} fusion(bf16[2,256,640]{2,1,0:T(8,128)(2,1)} %collective-permute-done.26, bf16[2,256,640]{2,1,0:T(8,128)(2,1)} %collective-permute-done.25, bf16[2,256,640]{2,1,0:T(8,128)(2,1)} %collective-permute-done.24, bf16[4,2,256,640]{3,2,1,0:T(8,128)(2,1)} %collective-permute-done.23, s32[]{:T(128)S(6)} %select_n.39, ...), kind=kLoop, calls=%fused_computation.1 | loop fusion | flops 3276800 | bytes 3932164 | tf_op jit(solution)/shard_map/convert_element_type | solution.py:340
  175.4 6.9 %collective-permute-start.16 = (bf16[2,4,2,128,256]{4,3,2,1,0:T(8,128)(2,1)S(1)}, bf16[2,4,2,128,256]{4,3,2,1,0:T(8,128)(2,1)}, u32[]{:S(2)}, u32[]{:S(2)}) collective-permute-start(bf16[2,4,2,128,256]{4,3,2,1,0:T(8,128)(2,1)S(1)} %pad_maximum_fusion), channel_id=1, source_target_pairs={{0,1},{1,0},{2,3},{3,2},{4,5},{5,4},{6,7},{7,6},{8,9},{9,8},{10,11... | collective-permute-start | bytes 3145736 | tf_op jit(solution)/shard_map/ppermute | solution.py:288
  189.4 2.6 %collective-permute-done.35 = f32[4608]{0:T(1024)S(1)} collective-permute-done((f32[4608]{0:T(1024)S(1)}, f32[4608]{0:T(1024)S(1)}, u32[]{:S(2)}, u32[]{:S(2)}) %collective-permute-start.35) | collective-permute-done | bytes 18464 | tf_op jit(solution)/shard_map/ppermute | solution.py:288
  192.0 3.1 %collective-permute-start.36 = (f32[4608]{0:T(1024)S(1)}, f32[4608]{0:T(1024)S(1)}, u32[]{:S(2)}, u32[]{:S(2)}) collective-permute-start(f32[4608]{0:T(1024)S(1)} %add.177), channel_id=1, source_target_pairs={{0,8},{4,12},{8,0},{12,4},{1,9},{5,13},{9,1},{13,5},{2,10},{6,14},... | collective-permute-start | bytes 55304 | tf_op jit(solution)/shard_map/ppermute | solution.py:288
  197.3 4.0 %collective-permute-done.28 = bf16[256,576]{1,0:T(8,128)(2,1)} collective-permute-done((bf16[256,576]{1,0:T(8,128)(2,1)}, bf16[256,576]{1,0:T(8,128)(2,1)}, u32[]{:S(2)}, u32[]{:S(2)}) %collective-permute-start.28) | collective-permute-done | bytes 294944 | tf_op jit(solution)/shard_map/ppermute | solution.py:288
  203.6 3.7 %place.1 = bf16[2,16,128,256]{3,2,1,0:T(8,128)(2,1)} custom-call(s32[3]{0:T(128)} %pad_add_fusion.place, bf16[2,4,2,128,256]{4,3,2,1,0:T(8,128)(2,1)} %get-tuple-element.18.mine, bf16[2,4,2,128,256]{4,3,2,1,0:T(8,128)(2,1)} %collective-permute-done.15.over, bf16[2,4,2,128,256]{4,3,2,1,0:T(8,128)(2,1)} %collective-permute-done.16.mates), custom_call_target="tpu_custom_call" | custom-call | flops 1000000 | bytes 8388608 | tf_op jit(solution)/shard_map/place/pallas_call | solution.py:272
  (122 shorter events, 46.3 us)
Async XLA Ops:
  6.6 15.7 %collective-permute-start.4 = (bf16[2,128,1024]{2,1,0:T(8,128)(2,1)}, bf16[2,128,1024]{2,1,0:T(8,128)(2,1)S(1)}, u32[]{:S(2)}, u32[]{:S(2)}) collective-permute-start(bf16[2,128,1024]{2,1,0:T(8,128)(2,1)} %get-tuple-element.17.refs_6_.refs_5_), channel_id=1, source_target_pairs={{0,4},{4,8},{8,12},{12,0},{1,5},{5,9},{9,13},{13,1},{2,6},{6,10},{... | collective-permute-start | bytes 1572872 | tf_op jit(solution)/shard_map/ppermute | solution.py:288
  8.6 15.3 %collective-permute-start.5 = (bf16[2,128,1024]{2,1,0:T(8,128)(2,1)}, bf16[2,128,1024]{2,1,0:T(8,128)(2,1)S(1)}, u32[]{:S(2)}, u32[]{:S(2)}) collective-permute-start(bf16[2,128,1024]{2,1,0:T(8,128)(2,1)} %get-tuple-element.17.refs_6_.refs_5_), channel_id=1, source_target_pairs={{0,12},{4,0},{8,4},{12,8},{1,13},{5,1},{9,5},{13,9},{2,14},{6,2},{... | collective-permute-start | bytes 1572872 | tf_op jit(solution)/shard_map/ppermute | solution.py:288
  9.9 28.2 %collective-permute-start.2 = (bf16[2,128,1536]{2,1,0:T(8,128)(2,1)}, bf16[2,128,1536]{2,1,0:T(8,128)(2,1)S(1)}, u32[]{:S(2)}, u32[]{:S(2)}) collective-permute-start(bf16[2,128,1536]{2,1,0:T(8,128)(2,1)} %get-tuple-element.16.refs_3_.refs_0_), channel_id=1, source_target_pairs={{0,4},{4,8},{8,12},{12,0},{1,5},{5,9},{9,13},{13,1},{2,6},{6,10},{... | collective-permute-start | bytes 2359304 | tf_op jit(solution)/shard_map/ppermute | solution.py:288
  17.1 24.9 %collective-permute-start.17 = (bf16[2,256,1024]{2,1,0:T(8,128)(2,1)}, bf16[2,256,1024]{2,1,0:T(8,128)(2,1)S(1)}, u32[]{:S(2)}, u32[]{:S(2)}) collective-permute-start(bf16[2,256,1024]{2,1,0:T(8,128)(2,1)} %get-tuple-element.21), channel_id=1, source_target_pairs={{0,2},{2,0},{1,3},{3,1},{4,6},{6,4},{5,7},{7,5},{8,10},{10,8},{9,1... | collective-permute-start | bytes 3145736 | tf_op jit(solution)/shard_map/ppermute | solution.py:288
  20.0 45.1 %collective-permute-start = (bf16[2,128,2048]{2,1,0:T(8,128)(2,1)}, bf16[2,128,2048]{2,1,0:T(8,128)(2,1)S(1)}, u32[]{:S(2)}, u32[]{:S(2)}) collective-permute-start(bf16[2,128,2048]{2,1,0:T(8,128)(2,1)} %get-tuple-element.15.refs_0_), channel_id=1, source_target_pairs={{0,4},{4,8},{8,12},{12,0},{1,5},{5,9},{9,13},{13,1},{2,6},{6,10},{... | collective-permute-start | bytes 3145736 | tf_op jit(solution)/shard_map/ppermute | solution.py:288
  22.3 45.7 %collective-permute-start.1 = (bf16[2,128,2048]{2,1,0:T(8,128)(2,1)}, bf16[2,128,2048]{2,1,0:T(8,128)(2,1)S(1)}, u32[]{:S(2)}, u32[]{:S(2)}) collective-permute-start(bf16[2,128,2048]{2,1,0:T(8,128)(2,1)} %get-tuple-element.15.refs_0_), channel_id=1, source_target_pairs={{0,12},{4,0},{8,4},{12,8},{1,13},{5,1},{9,5},{13,9},{2,14},{6,2},{... | collective-permute-start | bytes 3145736 | tf_op jit(solution)/shard_map/ppermute | solution.py:288
  23.9 38.3 %collective-permute-start.3 = (bf16[2,128,1536]{2,1,0:T(8,128)(2,1)S(1)}, bf16[2,128,1536]{2,1,0:T(8,128)(2,1)S(1)}, u32[]{:S(2)}, u32[]{:S(2)}) collective-permute-start(bf16[2,128,1536]{2,1,0:T(8,128)(2,1)S(1)} %copy-done.14), channel_id=1, source_target_pairs={{0,12},{4,0},{8,4},{12,8},{1,13},{5,1},{9,5},{13,9},{2,14},{6,2},{... | collective-permute-start | bytes 2359304 | tf_op jit(solution)/shard_map/ppermute | solution.py:288
  38.2 66.8 %collective-permute-start.13 = (bf16[256,4608]{1,0:T(8,128)(2,1)}, bf16[256,4608]{1,0:T(8,128)(2,1)}, u32[]{:S(2)}, u32[]{:S(2)}) collective-permute-start(bf16[256,4608]{1,0:T(8,128)(2,1)} %refs_15_.1), channel_id=1, source_target_pairs={{0,18},{2,16},{16,2},{18,0},{1,19},{3,17},{17,3},{19,1},{4,22},{6,... | collective-permute-start | bytes 7077896 | tf_op jit(solution)/shard_map/ppermute | solution.py:288
  42.0 25.9 %collective-permute-start.10 = (bf16[128,1024]{1,0:T(8,128)(2,1)S(1)}, bf16[128,1024]{1,0:T(8,128)(2,1)S(1)}, u32[]{:S(2)}, u32[]{:S(2)}) collective-permute-start(bf16[128,1024]{1,0:T(8,128)(2,1)S(1)} %slice_bitcast_fusion.9), channel_id=1, source_target_pairs={{0,4},{4,8},{8,12},{12,0},{1,5},{5,9},{9,13},{13,1},{2,6},{6,10},{... | collective-permute-start | bytes 786440 | tf_op jit(solution)/shard_map/ppermute | solution.py:288
  62.2 19.7 %collective-permute-start.18 = (bf16[2,256,1024]{2,1,0:T(8,128)(2,1)S(1)}, bf16[2,256,1024]{2,1,0:T(8,128)(2,1)S(1)}, u32[]{:S(2)}, u32[]{:S(2)}) collective-permute-start(bf16[2,256,1024]{2,1,0:T(8,128)(2,1)S(1)} %pad_maximum_fusion.1), channel_id=1, source_target_pairs={{0,1},{1,0},{2,3},{3,2},{4,5},{5,4},{6,7},{7,6},{8,9},{9,8},{10,11... | collective-permute-start | bytes 3145736 | tf_op jit(solution)/shard_map/ppermute | solution.py:288
  65.1 8.4 %collective-permute-start.11 = (bf16[128,1024]{1,0:T(8,128)(2,1)S(1)}, bf16[128,1024]{1,0:T(8,128)(2,1)S(1)}, u32[]{:S(2)}, u32[]{:S(2)}) collective-permute-start(bf16[128,1024]{1,0:T(8,128)(2,1)S(1)} %slice_bitcast_fusion.8), channel_id=1, source_target_pairs={{0,12},{4,0},{8,4},{12,8},{1,13},{5,1},{9,5},{13,9},{2,14},{6,2},{... | collective-permute-start | bytes 786440 | tf_op jit(solution)/shard_map/ppermute | solution.py:288
  67.9 11.8 %collective-permute-start.8 = (bf16[128,1536]{1,0:T(8,128)(2,1)S(1)}, bf16[128,1536]{1,0:T(8,128)(2,1)S(1)}, u32[]{:S(2)}, u32[]{:S(2)}) collective-permute-start(bf16[128,1536]{1,0:T(8,128)(2,1)S(1)} %slice_bitcast_fusion.3), channel_id=1, source_target_pairs={{0,4},{4,8},{8,12},{12,0},{1,5},{5,9},{9,13},{13,1},{2,6},{6,10},{... | collective-permute-start | bytes 1179656 | tf_op jit(solution)/shard_map/ppermute | solution.py:288
  68.6 13.3 %collective-permute-start.9 = (bf16[128,1536]{1,0:T(8,128)(2,1)S(1)}, bf16[128,1536]{1,0:T(8,128)(2,1)S(1)}, u32[]{:S(2)}, u32[]{:S(2)}) collective-permute-start(bf16[128,1536]{1,0:T(8,128)(2,1)S(1)} %slice_bitcast_fusion.2), channel_id=1, source_target_pairs={{0,12},{4,0},{8,4},{12,8},{1,13},{5,1},{9,5},{13,9},{2,14},{6,2},{... | collective-permute-start | bytes 1179656 | tf_op jit(solution)/shard_map/ppermute | solution.py:288
  73.5 21.3 %collective-permute-start.6 = (bf16[128,2048]{1,0:T(8,128)(2,1)S(1)}, bf16[128,2048]{1,0:T(8,128)(2,1)S(1)}, u32[]{:S(2)}, u32[]{:S(2)}) collective-permute-start(bf16[128,2048]{1,0:T(8,128)(2,1)S(1)} %slice_bitcast_fusion.1), channel_id=1, source_target_pairs={{0,4},{4,8},{8,12},{12,0},{1,5},{5,9},{9,13},{13,1},{2,6},{6,10},{... | collective-permute-start | bytes 1572872 | tf_op jit(solution)/shard_map/ppermute | solution.py:288
  79.7 15.1 %collective-permute-start.7 = (bf16[128,2048]{1,0:T(8,128)(2,1)S(1)}, bf16[128,2048]{1,0:T(8,128)(2,1)S(1)}, u32[]{:S(2)}, u32[]{:S(2)}) collective-permute-start(bf16[128,2048]{1,0:T(8,128)(2,1)S(1)} %slice_bitcast_fusion), channel_id=1, source_target_pairs={{0,12},{4,0},{8,4},{12,8},{1,13},{5,1},{9,5},{13,9},{2,14},{6,2},{... | collective-permute-start | bytes 1572872 | tf_op jit(solution)/shard_map/ppermute | solution.py:288
  93.4 30.7 %collective-permute-start.23 = (bf16[4,2,256,640]{3,2,1,0:T(8,128)(2,1)}, bf16[4,2,256,640]{3,2,1,0:T(8,128)(2,1)}, u32[]{:S(2)}, u32[]{:S(2)}) collective-permute-start(bf16[4,2,256,640]{3,2,1,0:T(8,128)(2,1)} %get-tuple-element.25), channel_id=1, source_target_pairs={{0,1},{1,0},{2,3},{3,2},{4,5},{5,4},{6,7},{7,6},{8,9},{9,8},{10,11... | collective-permute-start | bytes 7864328 | tf_op jit(solution)/shard_map/ppermute | solution.py:288
  104.5 25.8 %collective-permute-start.12 = (bf16[256,4608]{1,0:T(8,128)(2,1)}, bf16[256,4608]{1,0:T(8,128)(2,1)}, u32[]{:S(2)}, u32[]{:S(2)}) collective-permute-start(bf16[256,4608]{1,0:T(8,128)(2,1)} %refs_15_.1), channel_id=1, source_target_pairs={{0,1},{1,0},{2,3},{3,2},{4,5},{5,4},{6,7},{7,6},{8,9},{9,8},{10,11... | collective-permute-start | bytes 7077896 | tf_op jit(solution)/shard_map/ppermute | solution.py:288
  105.0 28.0 %collective-permute-start.14 = (bf16[256,4608]{1,0:T(8,128)(2,1)}, bf16[256,4608]{1,0:T(8,128)(2,1)}, u32[]{:S(2)}, u32[]{:S(2)}) collective-permute-start(bf16[256,4608]{1,0:T(8,128)(2,1)} %collective-permute-done.13.refs_17_), channel_id=1, source_target_pairs={{0,1},{1,0},{2,3},{3,2},{4,5},{5,4},{6,7},{7,6},{8,9},{9,8},{10,11... | collective-permute-start | bytes 7077896 | tf_op jit(solution)/shard_map/ppermute | solution.py:288
  113.5 18.4 %collective-permute-start.20 = (bf16[2,256,512]{2,1,0:T(8,128)(2,1)}, bf16[2,256,512]{2,1,0:T(8,128)(2,1)}, u32[]{:S(2)}, u32[]{:S(2)}) collective-permute-start(bf16[2,256,512]{2,1,0:T(8,128)(2,1)} %get-tuple-element.33), channel_id=1, source_target_pairs={{0,32},{32,64},{64,96},{96,0},{1,33},{33,65},{65,97},{97,1},{2,34}... | collective-permute-start | bytes 1572872 | tf_op jit(solution)/shard_map/ppermute | solution.py:288
  122.5 6.6 %collective-permute-start.32 = (f32[4608]{0:T(1024)S(1)}, f32[4608]{0:T(1024)S(1)}, u32[]{:S(2)}, u32[]{:S(2)}) collective-permute-start(f32[4608]{0:T(1024)S(1)} %add.173), channel_id=1, source_target_pairs={{0,32},{32,0},{64,96},{96,64},{1,33},{33,1},{65,97},{97,65},{2,34}... | collective-permute-start | bytes 55304 | tf_op jit(solution)/shard_map/ppermute | solution.py:288
  124.1 27.1 %collective-permute-start.21 = (bf16[2,256,512]{2,1,0:T(8,128)(2,1)}, bf16[2,256,512]{2,1,0:T(8,128)(2,1)}, u32[]{:S(2)}, u32[]{:S(2)}) collective-permute-start(bf16[2,256,512]{2,1,0:T(8,128)(2,1)} %get-tuple-element.35), channel_id=1, source_target_pairs={{0,96},{32,0},{64,32},{96,64},{1,97},{33,1},{65,33},{97,65},{2,98}... | collective-permute-start | bytes 1572872 | tf_op jit(solution)/shard_map/ppermute | solution.py:288
  129.1 24.2 %collective-permute-start.22 = (bf16[2,256,512]{2,1,0:T(8,128)(2,1)}, bf16[2,256,512]{2,1,0:T(8,128)(2,1)}, u32[]{:S(2)}, u32[]{:S(2)}) collective-permute-start(bf16[2,256,512]{2,1,0:T(8,128)(2,1)} %get-tuple-element.34), channel_id=1, source_target_pairs={{0,64},{32,96},{64,0},{96,32},{1,65},{33,97},{65,1},{97,33},{2,66}... | collective-permute-start | bytes 1572872 | tf_op jit(solution)/shard_map/ppermute | solution.py:288
  130.3 31.7 %collective-permute-start.24 = (bf16[2,256,640]{2,1,0:T(8,128)(2,1)}, bf16[2,256,640]{2,1,0:T(8,128)(2,1)}, u32[]{:S(2)}, u32[]{:S(2)}) collective-permute-start(bf16[2,256,640]{2,1,0:T(8,128)(2,1)} %get-tuple-element.30), channel_id=1, source_target_pairs={{0,32},{32,64},{64,96},{96,0},{1,33},{33,65},{65,97},{97,1},{2,34}... | collective-permute-start | bytes 1966088 | tf_op jit(solution)/shard_map/ppermute | solution.py:288
  132.0 30.0 %collective-permute-start.25 = (bf16[2,256,640]{2,1,0:T(8,128)(2,1)}, bf16[2,256,640]{2,1,0:T(8,128)(2,1)}, u32[]{:S(2)}, u32[]{:S(2)}) collective-permute-start(bf16[2,256,640]{2,1,0:T(8,128)(2,1)} %get-tuple-element.32), channel_id=1, source_target_pairs={{0,96},{32,0},{64,32},{96,64},{1,97},{33,1},{65,33},{97,65},{2,98}... | collective-permute-start | bytes 1966088 | tf_op jit(solution)/shard_map/ppermute | solution.py:288
  133.0 36.7 %collective-permute-start.26 = (bf16[2,256,640]{2,1,0:T(8,128)(2,1)S(1)}, bf16[2,256,640]{2,1,0:T(8,128)(2,1)}, u32[]{:S(2)}, u32[]{:S(2)}) collective-permute-start(bf16[2,256,640]{2,1,0:T(8,128)(2,1)S(1)} %get-tuple-element.31), channel_id=1, source_target_pairs={{0,64},{32,96},{64,0},{96,32},{1,65},{33,97},{65,1},{97,33},{2,66}... | collective-permute-start | bytes 1966088 | tf_op jit(solution)/shard_map/ppermute | solution.py:288
  151.3 22.9 %collective-permute-start.15 = (bf16[2,4,2,128,256]{4,3,2,1,0:T(8,128)(2,1)}, bf16[2,4,2,128,256]{4,3,2,1,0:T(8,128)(2,1)}, u32[]{:S(2)}, u32[]{:S(2)}) collective-permute-start(bf16[2,4,2,128,256]{4,3,2,1,0:T(8,128)(2,1)} %get-tuple-element.19), channel_id=1, source_target_pairs={{0,2},{2,0},{1,3},{3,1},{4,6},{6,4},{5,7},{7,5},{8,10},{10,8},{9,1... | collective-permute-start | bytes 3145736 | tf_op jit(solution)/shard_map/ppermute | solution.py:288
  153.3 33.8 %collective-permute-start.33 = (f32[4608]{0:T(1024)S(1)}, f32[4608]{0:T(1024)S(1)}, u32[]{:S(2)}, u32[]{:S(2)}) collective-permute-start(f32[4608]{0:T(1024)S(1)} %add.174), channel_id=1, source_target_pairs={{0,64},{32,96},{64,0},{96,32},{1,65},{33,97},{65,1},{97,33},{2,66}... | collective-permute-start | bytes 55304 | tf_op jit(solution)/shard_map/ppermute | solution.py:288
  175.4 28.2 %collective-permute-start.16 = (bf16[2,4,2,128,256]{4,3,2,1,0:T(8,128)(2,1)S(1)}, bf16[2,4,2,128,256]{4,3,2,1,0:T(8,128)(2,1)}, u32[]{:S(2)}, u32[]{:S(2)}) collective-permute-start(bf16[2,4,2,128,256]{4,3,2,1,0:T(8,128)(2,1)S(1)} %pad_maximum_fusion), channel_id=1, source_target_pairs={{0,1},{1,0},{2,3},{3,2},{4,5},{5,4},{6,7},{7,6},{8,9},{9,8},{10,11... | collective-permute-start | bytes 3145736 | tf_op jit(solution)/shard_map/ppermute | solution.py:288
  183.1 14.2 %collective-permute-start.27 = (bf16[256,576]{1,0:T(8,128)(2,1)}, bf16[256,576]{1,0:T(8,128)(2,1)S(1)}, u32[]{:S(2)}, u32[]{:S(2)}) collective-permute-start(bf16[256,576]{1,0:T(8,128)(2,1)} %get-tuple-element.38), channel_id=1, source_target_pairs={{0,16},{16,0},{1,17},{17,1},{2,18},{18,2},{3,19},{19,3},{4,20},{20... | collective-permute-start | bytes 884744 | tf_op jit(solution)/shard_map/ppermute | solution.py:288
  183.5 13.8 %collective-permute-start.29 = (bf16[256,576]{1,0:T(8,128)(2,1)}, bf16[256,576]{1,0:T(8,128)(2,1)}, u32[]{:S(2)}, u32[]{:S(2)}) collective-permute-start(bf16[256,576]{1,0:T(8,128)(2,1)} %get-tuple-element.39), channel_id=1, source_target_pairs={{0,18},{2,16},{16,2},{18,0},{1,19},{3,17},{17,3},{19,1},{4,22},{6,... | collective-permute-start | bytes 884744 | tf_op jit(solution)/shard_map/ppermute | solution.py:288
  186.1 15.1 %collective-permute-start.28 = (bf16[256,576]{1,0:T(8,128)(2,1)}, bf16[256,576]{1,0:T(8,128)(2,1)}, u32[]{:S(2)}, u32[]{:S(2)}) collective-permute-start(bf16[256,576]{1,0:T(8,128)(2,1)} %slice_bitcast_fusion.5), channel_id=1, source_target_pairs={{0,2},{2,0},{1,3},{3,1},{4,6},{6,4},{5,7},{7,5},{8,10},{10,8},{9,1... | collective-permute-start | bytes 884744 | tf_op jit(solution)/shard_map/ppermute | solution.py:288
  192.0 4.7 %collective-permute-start.36 = (f32[4608]{0:T(1024)S(1)}, f32[4608]{0:T(1024)S(1)}, u32[]{:S(2)}, u32[]{:S(2)}) collective-permute-start(f32[4608]{0:T(1024)S(1)} %add.177), channel_id=1, source_target_pairs={{0,8},{4,12},{8,0},{12,4},{1,9},{5,13},{9,1},{13,5},{2,10},{6,14},... | collective-permute-start | bytes 55304 | tf_op jit(solution)/shard_map/ppermute | solution.py:288
  (26 other events, 277.4 us)

commit v2 on v1

v2 whole, which is shorter than its diff:
```python
import functools
import math

import jax
import jax.numpy as jnp
from jax import lax
from jax.experimental import pallas as pl
from jax.experimental.pallas import tpu as pltpu
from jax.sharding import Mesh
from jax.sharding import PartitionSpec as P

Z, YL, X, YH, C = AXES = ("dp_0", "dp_1", "tensor_0", "tensor_1", "tensor_2")
DP = (Z, YL)
TENSOR = (X, YH, C)
BF16 = jnp.bfloat16
F32 = jnp.float32

PIECES = (((0, 256),), ((256, 512),), ((768, 384),))
SIZES = tuple(sum(size for _, size in runs) for runs in PIECES)
SUMS = ((0,), (1,), (2,))
RELATIVE = (0, -1, 1, 2)


def ring(step, size=4):
    return [(i, (i + step) % size) for i in range(size)]


def swap(size=2):
    return [(i, size - 1 - i) for i in range(size)]


def params(semantics, mib=28):
    return pltpu.CompilerParams(dimension_semantics=semantics, vmem_limit_bytes=mib * 1024 * 1024)


def cost(flops, moved):
    return pl.CostEstimate(flops=flops, bytes_accessed=moved, transcendentals=0)


def nt(lhs, rhs):
    return lax.dot_general(lhs, rhs, (((1,), (1,)), ((), ())), preferred_element_type=F32)


def near(position, j):
    if not isinstance(j, int):
        offset = jnp.where(j == 1, 3, jnp.where(j == 2, 1, jnp.where(j == 3, 2, 0)))
    else:
        offset = RELATIVE[j] % 4
    return lax.rem(position + offset, 4)


def norm_kernel(width, values, upstream, gains, *outs):
    pieces, total, acc = outs[:-2], outs[-2], outs[-1]

    @pl.when((pl.program_id(0) == 0) & (pl.program_id(1) == 0))
    def _():
        acc[...] = jnp.zeros_like(acc)

    v = values[0].astype(F32)
    u = upstream[0].astype(F32)
    inverse = lax.rsqrt(jnp.mean(v * v, axis=-1, keepdims=True) + 1e-06)
    n = v * inverse
    acc[...] += jnp.sum((u * n).reshape(-1, 8, u.shape[-1]), axis=0)
    total[...] = jnp.sum(acc[...], axis=0, keepdims=True)
    w = u * gains[...][None, :]
    back = (inverse * (w - n * jnp.mean(w * n, axis=-1, keepdims=True))).astype(BF16)
    for runs, out in zip(PIECES, pieces):
        at = 0
        for z in range(4):
            for start, size in runs:
                out[0, :, at : at + size] = back[:, z * width + start : z * width + start + size]
                at += size


def norm_pieces(projected, out_grad, gains, step=64):
    micro, rows, cols = projected.shape
    block = pl.BlockSpec((1, step, cols), lambda m, i: (m, i, 0))
    return pl.pallas_call(
        functools.partial(norm_kernel, cols // 4),
        grid=(micro, rows // step),
        in_specs=[block, block, pl.BlockSpec((cols,), lambda m, i: (0,))],
        out_specs=[pl.BlockSpec((1, step, 4 * s), lambda m, i: (m, i, 0)) for s in SIZES]
        + [pl.BlockSpec((1, cols), lambda m, i: (0, 0))],
        out_shape=[jax.ShapeDtypeStruct((micro, rows, 4 * s), BF16) for s in SIZES]
        + [jax.ShapeDtypeStruct((1, cols), F32)],
        scratch_shapes=[pltpu.VMEM((8, cols), F32)],
        compiler_params=params(("arbitrary", "arbitrary"), 63),
        cost_estimate=cost(16 * micro * rows * cols, 6 * micro * rows * cols),
        name="norm_back",
    )(projected, out_grad, gains)


def turn_kernel(place, rows, out):
    heads = rows.shape[-1]
    eye = (
        lax.broadcasted_iota(jnp.int32, (heads, heads), 0)
        == lax.broadcasted_iota(jnp.int32, (heads, heads), 1)
    ).astype(BF16)
    taken = [rows[m, near(place[0], j), 0] for j in range(4) for m in range(rows.shape[0])]
    out[0] = nt(eye, jnp.concatenate(taken, axis=0)).astype(BF16)


def turned(attention, place, across):
    micro, rows, heads = attention.shape
    each = rows // 16
    shape = (2, heads, 4 * micro * each)
    return pl.pallas_call(
        turn_kernel,
        grid_spec=pltpu.PrefetchScalarGridSpec(
            num_scalar_prefetch=1,
            grid=(2,),
            in_specs=[
                pl.BlockSpec(
                    (micro, 4, 1, each, heads),
                    lambda i, p: (0, 0, (p[1] ^ across) * 2 + (p[2] ^ i), 0, 0),
                )
            ],
            out_specs=pl.BlockSpec((1,) + shape[1:], lambda i, p: (i, 0, 0)),
        ),
        out_shape=jax.ShapeDtypeStruct(shape, BF16),
        compiler_params=params(("arbitrary",)),
        cost_estimate=cost(4 * heads * heads * shape[2], 8 * heads * shape[2]),
        name="turn",
    )(place, attention.reshape(micro, 4, 4, each, heads))


def data_kernel(plan, *refs):
    acc, refs = refs[-1], list(refs[:-1])
    step = pl.program_id(0)
    sides = []
    for pieces, number in plan:
        parts = []
        for _ in pieces:
            take, refs = refs[:number], refs[number:]
            parts.append(jnp.concatenate([r[...].reshape(-1, r.shape[-1]) for r in take], axis=0))
        sides.append(parts[0] if len(parts) == 1 else jnp.concatenate(parts, axis=1))
    weights, out = refs[:2], refs[2]

    @pl.when(step == 0)
    def _():
        acc[...] = jnp.zeros_like(acc)

    for h, w in enumerate(weights):
        at = 0
        for (pieces, _), lhs in zip(plan, sides):
            start = PIECES[pieces[0]][0][0]
            columns = slice(start, start + lhs.shape[1])
            acc[h, at : at + lhs.shape[0]] += nt(lhs, w[:, columns])
            at += lhs.shape[0]

    @pl.when(step == 3)
    def _():
        out[...] = acc[...].astype(BF16).reshape(out.shape)


def data_grad(plan, weights):
    flat = [a for _, arrays in plan for piece in arrays for a in piece]
    width = weights[0].shape[1] // 4
    rows = sum(sum(math.prod(a.shape[:-1]) for a in arrays[0]) for _, arrays in plan)

    def rows_spec(a):
        size = a.shape[-1] // 4
        if len(a.shape) == 3:
            return pl.BlockSpec(a.shape[:2] + (size,), lambda t: (0, 0, t))
        return pl.BlockSpec((a.shape[0], size), lambda t: (0, t))

    shape = (2, rows // 256, 2, 128, 256)
    flops = sum(
        2 * math.prod(a.shape) * 512 for _, arrays in plan for piece in arrays for a in piece
    )
    return pl.pallas_call(
        functools.partial(data_kernel, [(k, len(a[0])) for k, a in plan]),
        grid=(4,),
        in_specs=[rows_spec(a) for a in flat] + [pl.BlockSpec((256, width), lambda t: (0, t))] * 2,
        out_specs=pl.BlockSpec(shape, lambda t: (0, 0, 0, 0, 0)),
        out_shape=jax.ShapeDtypeStruct(shape, BF16),
        scratch_shapes=[pltpu.VMEM((2, rows, 256), F32)],
        compiler_params=params(("arbitrary",), 63),
        cost_estimate=cost(flops, 16 * 1024 * width),
        name="data_grad",
    )(*flat, *weights)


def weight_sum(pieces, groups):
    sizes = [piece[0].shape[2] // 4 for piece in pieces]
    total = sum(sizes)
    zs = 1 if total % 512 == 0 else 2
    out = pl.BlockSpec((zs, 2, 256, total), lambda i: (i, 0, 0, 0))
    specs = []
    for size in sizes:
        specs += [pl.BlockSpec((2, 128, zs * size), lambda i: (0, 0, i))] * 3
        specs += [pl.BlockSpec((128, zs * size), lambda i: (0, i))] * 2
    heads = [h for group in groups for h in group]
    specs += [pl.BlockSpec((1, 256, 1024), lambda i, n=n: (n, 0, 0)) for _, n in heads]

    def kernel(*refs):
        ins, outs = refs[: -len(groups)], refs[-len(groups) :]
        at = 0
        for k, size in enumerate(sizes):
            rows = jnp.concatenate(
                [r[...].reshape(-1, zs * size) for r in ins[5 * k : 5 * k + 5]], axis=0
            )
            for h, block in enumerate(ins[5 * len(sizes) :]):
                part = jnp.dot(block[0], rows, preferred_element_type=F32).astype(BF16)
                for n in range(zs):
                    outs[h // 2][n, h % 2, :, at : at + size] = part[:, n * size : (n + 1) * size]
            at += size

    return pl.pallas_call(
        kernel,
        grid=(4 // zs,),
        in_specs=specs,
        out_specs=[out] * len(groups),
        out_shape=[jax.ShapeDtypeStruct((4, 2, 256, total), BF16)] * len(groups),
        compiler_params=params(("arbitrary",)),
        cost_estimate=cost(2 * len(heads) * 1024 * 1024 * total, 20 * 1024 * total),
        name="weight_sum",
    )(*[a for piece in pieces for a in piece], *[h for h, _ in heads])


def place_kernel(place, mine, over, mates, out):
    for j in range(4):
        for h, block in enumerate((mine.at[0], mates.at[0], over.at[0], mates.at[1])):
            at = near(place[0], j) * 4 + (place[1] ^ (h // 2)) * 2 + (place[2] ^ (h % 2))
            out[:, pl.ds(at, 1)] = block[j][:, None]


def placed(place, blocks):
    mine, over, mates = blocks
    shape = mine.shape[1:]
    one = pl.BlockSpec((1,) + shape, lambda i, p: (0, 0, 0, 0, 0))
    two = pl.BlockSpec((2,) + shape, lambda i, p: (0, 0, 0, 0, 0))
    return pl.pallas_call(
        place_kernel,
        grid_spec=pltpu.PrefetchScalarGridSpec(
            num_scalar_prefetch=1,
            grid=(1,),
            in_specs=[one, one, two],
            out_specs=pl.BlockSpec((2, 16, 128, 256), lambda i, p: (0, 0, 0, 0)),
        ),
        out_shape=jax.ShapeDtypeStruct((2, 16, 128, 256), BF16),
        compiler_params=params(("arbitrary",)),
        cost_estimate=cost(1000000, 16 * 1024 * 1024 // 2),
        name="place",
    )(place, mine, over, mates)


def moved(value, axis, pairs):
    return lax.ppermute(value, axis, pairs)


def per_device(projected, out_grad, attention, w_out, gains, main_out, main_gains):
    micro, own_rows, cols = projected.shape
    tokens_all = micro * own_rows * lax.axis_size(AXES)
    factor = 1.0 / math.sqrt(tokens_all)
    here, low = lax.axis_index(Z), lax.axis_index(YL)
    place = jnp.stack([lax.axis_index(X), lax.axis_index(YH), lax.axis_index(C)])

    *own, gain = norm_pieces(projected, out_grad, gains)
    left = [moved(p, X, ring(1)) for p in own]
    right = [moved(p, X, ring(-1)) for p in own]
    far = []
    for k in range(len(own)):
        a, b = left[k][0], right[k][1]
        far.append((moved(a, X, ring(1)), moved(b, X, ring(-1))))

    def exchanged(mine, over):
        over = moved(over, YH, swap())
        mates = jnp.stack([mine[1], over[1]])
        return mine, over, moved(mates, C, swap())

    over = turned(attention, place, 1)
    heads = exchanged(turned(attention, place, 0), over)

    over = moved(w_out, (YL, YH), swap(4))
    weights = (w_out, moved(w_out, C, swap()), over, moved(over, C, swap()))

    for axis, bit in ((YH, 1), (YL, 1), (Z, 1), (Z, 2), (C, 1), (X, 1), (X, 2)):
        pairs = [(i, i ^ bit) for i in range(lax.axis_size(axis))]
        gain = gain + moved(gain, axis, pairs)
    new_gains = main_gains + factor * gain[0]

    plan = [
        (tuple(range(len(own))), [(own[k], left[k], right[k]) for k in range(len(own))]),
        (tuple(range(len(own))), far),
    ]
    over = data_grad(plan, weights[2:])
    mine = data_grad(plan, weights[:2])
    grad = placed(place, exchanged(mine, over))

    def reduced(k):
        pieces = [(own[i], left[i], right[i], *far[i]) for i in SUMS[k]]
        mine, over, mates = heads
        keep, send = weight_sum(pieces, [((mine, 0), (over, 0)), ((mates, 0), (mates, 1))])
        other = moved(send, C, swap())

        def block(step):
            at = lax.rem(here + step + 4, 4)
            a = lax.dynamic_index_in_dim(keep, at, 0, keepdims=False).astype(F32)
            return a + lax.dynamic_index_in_dim(other, at, 0, keepdims=False).astype(F32)

        blocks = [block(step).astype(BF16) for step in (1, -1, 2)]
        got = [moved(value, Z, ring(step)) for value, step in zip(blocks, (1, -1, 2))]
        return (block(0) + sum(g.astype(F32) for g in got)).astype(BF16)

    whole = jnp.concatenate([reduced(k) for k in range(len(SUMS))], axis=2)
    first, second = whole[:, :, : cols // 8], whole[:, :, cols // 8 :]
    ours, theirs = jnp.where(low == 0, first, second), jnp.where(low == 0, second, first)
    total = ours[0].astype(F32)
    for value, axes, pairs in ((theirs[0], YL, swap()), (ours[1], YH, swap()), (theirs[1], (YL, YH), swap(4))):
        got = moved(value, axes, pairs)
        total += got.astype(F32)
    new_out = (main_out.T + factor * total.T).T
    return (grad.reshape(attention.shape), new_out, new_gains)


def solution(mesh):
    torus = Mesh(mesh.devices.reshape(4, 2, 4, 2, 2), AXES)

    return jax.shard_map(
        per_device,
        mesh=torus,
        in_specs=(
            P(None, AXES, None),
            P(None, AXES, None),
            P(None, DP, TENSOR),
            P(TENSOR, None),
            P(),
            P(TENSOR, DP),
            P(),
        ),
        out_specs=(P(None, DP, TENSOR), P(TENSOR, DP), P()),
        check_vma=False,
    )
```

time: 208 us -> 242 us (1.16)
  waiting for transfers between devices: 73.8 us -> 99.9 us
  starting transfers between devices: 56.9 us -> 59.7 us
  other arithmetic: 14.5 us -> 17.1 us
    ppermute x37 -> x41, waiting for transfers between devices: 73.8 us -> 99.9 us  [moved(): return lax.ppermute(value, axis, pairs)]
    pallas_call x1 -> x2, Pallas kernels: 17.4 us -> 21.1 us  [data_grad(): pl.pallas_call(functools.partial(data_kernel, [(k, len(a[0])) for k, a in...]
    ppermute x37 -> x41, starting transfers between devices: 56.9 us -> 59.7 us  [moved(): return lax.ppermute(value, axis, pairs)]
    pallas_call x1 -> x2, Pallas kernels: 5.69 us -> 3.5 us  [turned(): pl.pallas_call(turn_kernel, grid_spec=pltpu.PrefetchScalarGridSpec(num_sc...]
    convert_element_type x2 -> x3, other arithmetic: 4.1 us -> 5.07 us  [reduced(): return (block(0) + sum((g.astype(F32) for g in got))).astype(BF16)]
    pallas_call x2 -> x3, Pallas kernels: 17.7 us -> 17.4 us  [weight_sum(): pl.pallas_call(kernel, grid=(4 // zs,), in_specs=specs, out_specs=[out] *...]
    unnamed x44 -> x56, local copies, waits for them, and re-layouts: 6.57 us -> 6.84 us
  transfers between devices with their start and end apart: 37 -> 41, of which waited for: 16 -> 14; matrix products, arithmetic and copies ran while one was open for 10% -> 9% of each run, Pallas kernels for 20% -> 19%
where the time goes in v2:
time: 242 us; the launch traced here: 240 us
  waiting for transfers between devices  99.9 us (41%)
  starting transfers between devices  59.7 us (25%)
  Pallas kernels  51.1 us (21%)
  other arithmetic  17.1 us (7%)
  local copies, waits for them, and re-layouts  11.1 us (5%)
    ppermute x41, waiting for transfers between devices, moved(): return lax.ppermute(value, axis, pairs)  99.9 us
    ppermute x41, starting transfers between devices, moved(): return lax.ppermute(value, axis, pairs)  59.7 us
    pallas_call x2, Pallas kernels, data_grad(): pl.pallas_call(functools.partial(data_kernel, [(k, len(a[0])) for k, a in...  21.1 us
    pallas_call x3, Pallas kernels, weight_sum(): pl.pallas_call(kernel, grid=(4 // zs,), in_specs=specs, out_specs=[out] *...  17.4 us
    convert_element_type x3, other arithmetic, reduced(): blocks = [block(step).astype(BF16) for step in (1, -1, 2)]  7.3 us
    unnamed x56, local copies, waits for them, and re-layouts  6.84 us
    pallas_call x1, Pallas kernels, norm_pieces(): pl.pallas_call(functools.partial(norm_kernel, cols // 4), grid=(micro, ro...  6.1 us
    convert_element_type x3, other arithmetic, reduced(): return (block(0) + sum((g.astype(F32) for g in got))).astype(BF16)  5.07 us
  transfers between devices with their start and end apart: 41, of which 14 were waited for; matrix products, arithmetic and copies ran while one was open for 9% of the time, Pallas kernels for 19%

profile of v2, /device:TPU:1, one launch (start us, length us, event | category | flops | bytes accessed | tf_op | source)
XLA Modules:
  0.0 240.0 jit_solution(18055102837759836556)
XLA Ops:
  4.5 3.7 %collective-permute-start.17 = (bf16[2,256,1024]{2,1,0:T(8,128)(2,1)}, bf16[2,256,1024]{2,1,0:T(8,128)(2,1)}, u32[]{:S(2)}, u32[]{:S(2)}) collective-permute-start(bf16[2,256,1024]{2,1,0:T(8,128)(2,1)} %turn.3), channel_id=1, source_target_pairs={{0,2},{2,0},{1,3},{3,1},{4,6},{6,4},{5,7},{7,5},{8,10},{10,8},{9,1... | collective-permute-start | bytes 3145736 | tf_op jit(solution)/shard_map/ppermute | solution.py:249
  8.2 6.1 %norm_back.1 = (bf16[2,128,1024]{2,1,0:T(8,128)(2,1)}, bf16[2,128,2048]{2,1,0:T(8,128)(2,1)}, bf16[2,128,1536]{2,1,0:T(8,128)(2,1)}, f32[1,4608]{1,0:T(1,128)}) custom-call(bf16[2,128,4608]{2,1,0:T(8,128)(2,1)} %values.1, bf16[2,128,4608]{2,1,0:T(8,128)(2,1)} %upstream.1, f32[4608]{0:T(1024)} %gains.1), custom_call_target="tpu_custom_call" | custom-call | flops 18874368 | bytes 7077888 | tf_op jit(solution)/shard_map/norm_back/pallas_call | solution.py:78
  21.2 29.5 %collective-permute-done.refs_1_ = bf16[2,128,1024]{2,1,0:T(8,128)(2,1)S(1)} collective-permute-done((bf16[2,128,1024]{2,1,0:T(8,128)(2,1)}, bf16[2,128,1024]{2,1,0:T(8,128)(2,1)S(1)}, u32[]{:S(2)}, u32[]{:S(2)}) %collective-permute-start) | collective-permute-done | bytes 524320 | tf_op jit(solution)/shard_map/ppermute | solution.py:249
  54.1 3.9 %collective-permute-start.18 = (bf16[2,256,1024]{2,1,0:T(8,128)(2,1)S(1)}, bf16[2,256,1024]{2,1,0:T(8,128)(2,1)S(1)}, u32[]{:S(2)}, u32[]{:S(2)}) collective-permute-start(bf16[2,256,1024]{2,1,0:T(8,128)(2,1)S(1)} %pad_maximum_fusion.1), channel_id=1, source_target_pairs={{0,1},{1,0},{2,3},{3,2},{4,5},{5,4},{6,7},{7,6},{8,9},{9,8},{10,11... | collective-permute-start | bytes 3145736 | tf_op jit(solution)/shard_map/ppermute | solution.py:249
  58.4 9.3 %collective-permute-done.4.refs_7_.refs_1_ = bf16[2,128,1536]{2,1,0:T(8,128)(2,1)S(1)} collective-permute-done((bf16[2,128,1536]{2,1,0:T(8,128)(2,1)}, bf16[2,128,1536]{2,1,0:T(8,128)(2,1)S(1)}, u32[]{:S(2)}, u32[]{:S(2)}) %collective-permute-start.4) | collective-permute-done | bytes 786464 | tf_op jit(solution)/shard_map/ppermute | solution.py:249
  69.6 9.3 %collective-permute-done.8.refs_11_.refs_3_ = bf16[128,2048]{1,0:T(8,128)(2,1)S(1)} collective-permute-done((bf16[128,2048]{1,0:T(8,128)(2,1)S(1)}, bf16[128,2048]{1,0:T(8,128)(2,1)S(1)}, u32[]{:S(2)}, u32[]{:S(2)}) %collective-permute-start.8) | collective-permute-done | bytes 524320 | tf_op jit(solution)/shard_map/ppermute | solution.py:249
  80.6 2.7 %collective-permute-start.11 = (bf16[128,1536]{1,0:T(8,128)(2,1)S(1)}, bf16[128,1536]{1,0:T(8,128)(2,1)S(1)}, u32[]{:S(2)}, u32[]{:S(2)}) collective-permute-start(bf16[128,1536]{1,0:T(8,128)(2,1)S(1)} %slice_bitcast_fusion.2), channel_id=1, source_target_pairs={{0,12},{4,0},{8,4},{12,8},{1,13},{5,1},{9,5},{13,9},{2,14},{6,2},{... | collective-permute-start | bytes 1179656 | tf_op jit(solution)/shard_map/ppermute | solution.py:249
  83.3 7.2 %weight_sum.4 = (bf16[4,2,256,512]{3,2,1,0:T(8,128)(2,1)S(1)}, bf16[4,2,256,512]{3,2,1,0:T(8,128)(2,1)}) custom-call(bf16[2,128,2048]{2,1,0:T(8,128)(2,1)S(1)} %copy-done.13, bf16[2,128,2048]{2,1,0:T(8,128)(2,1)S(1)} %collective-permute-done.2.refs_4_.refs_1_, bf16[2,128,2048]{2,1,0:T(8,128)(2,1)S(1)} %collective-permute-done.3.refs_5_.refs_2_, ...), custom_call_target="tpu_custom_call" | custom-call | flops 4294967296 | bytes 10485760 | tf_op jit(solution)/shard_map/weight_sum/pallas_call | solution.py:209
  90.5 6.3 %collective-permute-start.23 = (bf16[4,2,256,512]{3,2,1,0:T(8,128)(2,1)}, bf16[4,2,256,512]{3,2,1,0:T(8,128)(2,1)}, u32[]{:S(2)}, u32[]{:S(2)}) collective-permute-start(bf16[4,2,256,512]{3,2,1,0:T(8,128)(2,1)} %get-tuple-element.19), channel_id=1, source_target_pairs={{0,1},{1,0},{2,3},{3,2},{4,5},{5,4},{6,7},{7,6},{8,9},{9,8},{10,11... | collective-permute-start | bytes 6291464 | tf_op jit(solution)/shard_map/ppermute | solution.py:249
  96.8 6.1 %collective-permute-done.13.refs_15_ = bf16[256,4608]{1,0:T(8,128)(2,1)} collective-permute-done((bf16[256,4608]{1,0:T(8,128)(2,1)}, bf16[256,4608]{1,0:T(8,128)(2,1)}, u32[]{:S(2)}, u32[]{:S(2)}) %collective-permute-start.13) | collective-permute-done | bytes 2359328 | tf_op jit(solution)/shard_map/ppermute | solution.py:249
  102.9 4.4 %collective-permute-start.14 = (bf16[256,4608]{1,0:T(8,128)(2,1)}, bf16[256,4608]{1,0:T(8,128)(2,1)}, u32[]{:S(2)}, u32[]{:S(2)}) collective-permute-start(bf16[256,4608]{1,0:T(8,128)(2,1)} %collective-permute-done.13.refs_15_), channel_id=1, source_target_pairs={{0,1},{1,0},{2,3},{3,2},{4,5},{5,4},{6,7},{7,6},{8,9},{9,8},{10,11... | collective-permute-start | bytes 7077896 | tf_op jit(solution)/shard_map/ppermute | solution.py:249
  107.6 2.5 %collective-permute-start.7 = (bf16[128,1024]{1,0:T(8,128)(2,1)S(1)}, bf16[128,1024]{1,0:T(8,128)(2,1)S(1)}, u32[]{:S(2)}, u32[]{:S(2)}) collective-permute-start(bf16[128,1024]{1,0:T(8,128)(2,1)S(1)} %slice_bitcast_fusion.8), channel_id=1, source_target_pairs={{0,12},{4,0},{8,4},{12,8},{1,13},{5,1},{9,5},{13,9},{2,14},{6,2},{... | collective-permute-start | bytes 786440 | tf_op jit(solution)/shard_map/ppermute | solution.py:249
  110.1 5.7 %weight_sum.5 = (bf16[4,2,256,384]{3,2,1,0:T(8,128)(2,1)S(1)}, bf16[4,2,256,384]{3,2,1,0:T(8,128)(2,1)}) custom-call(bf16[2,128,1536]{2,1,0:T(8,128)(2,1)S(1)} %copy-done.14, bf16[2,128,1536]{2,1,0:T(8,128)(2,1)S(1)} %collective-permute-done.4.refs_7_.refs_1_, bf16[2,128,1536]{2,1,0:T(8,128)(2,1)S(1)} %collective-permute-done.5.refs_8_.refs_2_, ...), custom_call_target="tpu_custom_call" | custom-call | flops 3221225472 | bytes 7864320 | tf_op jit(solution)/shard_map/weight_sum/pallas_call | solution.py:209
  117.6 4.5 %weight_sum.3 = (bf16[4,2,256,256]{3,2,1,0:T(8,128)(2,1)S(1)}, bf16[4,2,256,256]{3,2,1,0:T(8,128)(2,1)}) custom-call(bf16[2,128,1024]{2,1,0:T(8,128)(2,1)S(1)} %copy-done.15, bf16[2,128,1024]{2,1,0:T(8,128)(2,1)S(1)} %collective-permute-done.refs_1_, bf16[2,128,1024]{2,1,0:T(8,128)(2,1)S(1)} %collective-permute-done.1.refs_2_, ...), custom_call_target="tpu_custom_call" | custom-call | flops 2147483648 | bytes 5242880 | tf_op jit(solution)/shard_map/weight_sum/pallas_call | solution.py:209
  122.2 2.9 %collective-permute-done.19 = bf16[4,2,256,256]{3,2,1,0:T(8,128)(2,1)} collective-permute-done((bf16[4,2,256,256]{3,2,1,0:T(8,128)(2,1)}, bf16[4,2,256,256]{3,2,1,0:T(8,128)(2,1)}, u32[]{:S(2)}, u32[]{:S(2)}) %collective-permute-start.19) | collective-permute-done | bytes 1048608 | tf_op jit(solution)/shard_map/ppermute | solution.py:249
  128.9 2.2 collective-permute-start.21
  131.1 2.4 %fusion.10 = (bf16[2,256,384]{2,1,0:T(8,128)(2,1)}, bf16[2,256,384]{2,1,0:T(8,128)(2,1)}, bf16[2,256,384]{2,1,0:T(8,128)(2,1)}) fusion(bf16[4,2,256,384]{3,2,1,0:T(8,128)(2,1)} %collective-permute-done.27, s32[]{:T(128)S(6)} %select_n.49, bf16[4,2,256,384]{3,2,1,0:T(8,128)(2,1)S(1)} %copy-done.5, s32[]{:T(128)S(6)} %select_n.51, s32[]{:T(128)S(6)} %select_n.50), kind=kLoop, calls=%fused_computation.31 | loop fusion | flops 2359296 | bytes 3538956 | tf_op jit(solution)/shard_map/convert_element_type | solution.py:302
  134.8 2.8 %fusion.6 = (bf16[2,256,512]{2,1,0:T(8,128)(2,1)}, bf16[2,256,512]{2,1,0:T(8,128)(2,1)}, bf16[2,256,512]{2,1,0:T(8,128)(2,1)}) fusion(bf16[4,2,256,512]{3,2,1,0:T(8,128)(2,1)} %collective-permute-done.23, s32[]{:T(128)S(6)} %select_n.49, bf16[4,2,256,512]{3,2,1,0:T(8,128)(2,1)S(1)} %get-tuple-element.18, s32[]{:T(128)S(6)} %select_n.51, s32[]{:T(128)S(6)} %select_n.50), kind=kLoop, calls=%fused_computation.21 | loop fusion | flops 3145728 | bytes 4718604 | tf_op jit(solution)/shard_map/convert_element_type | solution.py:302
  140.3 10.5 %data_grad.3 = bf16[2,4,2,128,256]{4,3,2,1,0:T(8,128)(2,1)} custom-call(bf16[2,128,1024]{2,1,0:T(8,128)(2,1)} %get-tuple-element.13.refs_0_, bf16[2,128,1024]{2,1,0:T(8,128)(2,1)} %copy-done.11, bf16[2,128,1024]{2,1,0:T(8,128)(2,1)} %copy-done.12, bf16[2,128,2048]{2,1,0:T(8,128)(2,1)} %get-tuple-element.14.refs_3_.refs_0_, bf16[2,128,2048]{2,1,0:T(8,128)(2,1)} %copy-done.7, ...), custom_call_target="tpu_custom_call" | custom-call | flops 4831838208 | bytes 18874368 | tf_op jit(solution)/shard_map/data_grad/pallas_call | solution.py:171
  151.5 2.6 %collective-permute-start.25 = (bf16[2,256,512]{2,1,0:T(8,128)(2,1)}, bf16[2,256,512]{2,1,0:T(8,128)(2,1)}, u32[]{:S(2)}, u32[]{:S(2)}) collective-permute-start(bf16[2,256,512]{2,1,0:T(8,128)(2,1)} %get-tuple-element.28), channel_id=1, source_target_pairs={{0,96},{32,0},{64,32},{96,64},{1,97},{33,1},{65,33},{97,65},{2,98}... | collective-permute-start | bytes 1572872 | tf_op jit(solution)/shard_map/ppermute | solution.py:249
  155.4 10.6 %data_grad.2.mine = bf16[2,4,2,128,256]{4,3,2,1,0:T(8,128)(2,1)} custom-call(bf16[2,128,1024]{2,1,0:T(8,128)(2,1)} %get-tuple-element.13.refs_0_, bf16[2,128,1024]{2,1,0:T(8,128)(2,1)} %copy-done.11, bf16[2,128,1024]{2,1,0:T(8,128)(2,1)} %copy-done.12, bf16[2,128,2048]{2,1,0:T(8,128)(2,1)} %get-tuple-element.14.refs_3_.refs_0_, ...), custom_call_target="tpu_custom_call" | custom-call | flops 4831838208 | bytes 18874368 | tf_op jit(solution)/shard_map/data_grad/pallas_call | solution.py:171
  169.0 7.8 %collective-permute-done.24 = bf16[2,256,512]{2,1,0:T(8,128)(2,1)} collective-permute-done((bf16[2,256,512]{2,1,0:T(8,128)(2,1)}, bf16[2,256,512]{2,1,0:T(8,128)(2,1)}, u32[]{:S(2)}, u32[]{:S(2)}) %collective-permute-start.24) | collective-permute-done | bytes 524320 | tf_op jit(solution)/shard_map/ppermute | solution.py:249
  176.8 7.6 %collective-permute-done.26 = bf16[2,256,512]{2,1,0:T(8,128)(2,1)} collective-permute-done((bf16[2,256,512]{2,1,0:T(8,128)(2,1)}, bf16[2,256,512]{2,1,0:T(8,128)(2,1)}, u32[]{:S(2)}, u32[]{:S(2)}) %collective-permute-start.26) | collective-permute-done | bytes 524320 | tf_op jit(solution)/shard_map/ppermute | solution.py:249
  189.4 2.4 collective-permute-start.16
  194.2 2.5 %collective-permute-start.32 = (bf16[256,576]{1,0:T(8,128)(2,1)}, bf16[256,576]{1,0:T(8,128)(2,1)}, u32[]{:S(2)}, u32[]{:S(2)}) collective-permute-start(bf16[256,576]{1,0:T(8,128)(2,1)} %slice_bitcast_fusion.5), channel_id=1, source_target_pairs={{0,2},{2,0},{1,3},{3,1},{4,6},{6,4},{5,7},{7,5},{8,10},{10,8},{9,1... | collective-permute-start | bytes 884744 | tf_op jit(solution)/shard_map/ppermute | solution.py:249
  197.2 13.0 %collective-permute-done.34 = f32[1,4608]{1,0:T(1,128)S(1)} collective-permute-done((f32[1,4608]{1,0:T(1,128)S(1)}, f32[1,4608]{1,0:T(1,128)S(1)}, u32[]{:S(2)}, u32[]{:S(2)}) %collective-permute-start.34) | collective-permute-done | bytes 18464 | tf_op jit(solution)/shard_map/ppermute | solution.py:249
  210.3 2.6 %collective-permute-done.35 = f32[1,4608]{1,0:T(1,128)S(1)} collective-permute-done((f32[1,4608]{1,0:T(1,128)S(1)}, f32[1,4608]{1,0:T(1,128)S(1)}, u32[]{:S(2)}, u32[]{:S(2)}) %collective-permute-start.35) | collective-permute-done | bytes 18464 | tf_op jit(solution)/shard_map/ppermute | solution.py:249
  213.0 2.6 %collective-permute-done.36 = f32[1,4608]{1,0:T(1,128)S(1)} collective-permute-done((f32[1,4608]{1,0:T(1,128)S(1)}, f32[1,4608]{1,0:T(1,128)S(1)}, u32[]{:S(2)}, u32[]{:S(2)}) %collective-permute-start.36) | collective-permute-done | bytes 18464 | tf_op jit(solution)/shard_map/ppermute | solution.py:249
  216.3 3.6 %collective-permute-done.37 = f32[1,4608]{1,0:T(1,128)S(1)} collective-permute-done((f32[1,4608]{1,0:T(1,128)S(1)}, f32[1,4608]{1,0:T(1,128)S(1)}, u32[]{:S(2)}, u32[]{:S(2)}) %collective-permute-start.37) | collective-permute-done | bytes 18464 | tf_op jit(solution)/shard_map/ppermute | solution.py:249
  219.9 4.3 %collective-permute-start.38 = (f32[1,4608]{1,0:T(1,128)S(1)}, f32[1,4608]{1,0:T(1,128)S(1)}, u32[]{:S(2)}, u32[]{:S(2)}) collective-permute-start(f32[1,4608]{1,0:T(1,128)S(1)} %add.227), channel_id=1, source_target_pairs={{0,1},{1,0},{2,3},{3,2},{4,5},{5,4},{6,7},{7,6},{8,9},{9,8},{10,11... | collective-permute-start | bytes 55304 | tf_op jit(solution)/shard_map/ppermute | solution.py:249
  225.2 2.6 %collective-permute-done.39 = f32[1,4608]{1,0:T(1,128)S(1)} collective-permute-done((f32[1,4608]{1,0:T(1,128)S(1)}, f32[1,4608]{1,0:T(1,128)S(1)}, u32[]{:S(2)}, u32[]{:S(2)}) %collective-permute-start.39) | collective-permute-done | bytes 18464 | tf_op jit(solution)/shard_map/ppermute | solution.py:249
  236.9 3.0 %place.1 = bf16[2,16,128,256]{3,2,1,0:T(8,128)(2,1)} custom-call(s32[3]{0:T(128)S(1)} %pad_add_fusion.place, bf16[2,4,2,128,256]{4,3,2,1,0:T(8,128)(2,1)S(1)} %copy-done.2, bf16[2,4,2,128,256]{4,3,2,1,0:T(8,128)(2,1)} %collective-permute-done.15.over, bf16[2,4,2,128,256]{4,3,2,1,0:T(8,128)(2,1)S(1)} %collective-permute-done.16.mates), custom_call_target="tpu_custom_call" | custom-call | flops 1000000 | bytes 8388608 | tf_op jit(solution)/shard_map/place/pallas_call | solution.py:233
  (147 shorter events, 51.8 us)
Async XLA Ops:
  4.5 47.6 %collective-permute-start.17 = (bf16[2,256,1024]{2,1,0:T(8,128)(2,1)}, bf16[2,256,1024]{2,1,0:T(8,128)(2,1)}, u32[]{:S(2)}, u32[]{:S(2)}) collective-permute-start(bf16[2,256,1024]{2,1,0:T(8,128)(2,1)} %turn.3), channel_id=1, source_target_pairs={{0,2},{2,0},{1,3},{3,1},{4,6},{6,4},{5,7},{7,5},{8,10},{10,8},{9,1... | collective-permute-start | bytes 3145736 | tf_op jit(solution)/shard_map/ppermute | solution.py:249
  14.3 39.8 %collective-permute-start.2 = (bf16[2,128,2048]{2,1,0:T(8,128)(2,1)}, bf16[2,128,2048]{2,1,0:T(8,128)(2,1)S(1)}, u32[]{:S(2)}, u32[]{:S(2)}) collective-permute-start(bf16[2,128,2048]{2,1,0:T(8,128)(2,1)} %get-tuple-element.14.refs_3_.refs_0_), channel_id=1, source_target_pairs={{0,4},{4,8},{8,12},{12,0},{1,5},{5,9},{9,13},{13,1},{2,6},{6,10},{... | collective-permute-start | bytes 3145736 | tf_op jit(solution)/shard_map/ppermute | solution.py:249
  15.5 35.2 %collective-permute-start = (bf16[2,128,1024]{2,1,0:T(8,128)(2,1)}, bf16[2,128,1024]{2,1,0:T(8,128)(2,1)S(1)}, u32[]{:S(2)}, u32[]{:S(2)}) collective-permute-start(bf16[2,128,1024]{2,1,0:T(8,128)(2,1)} %get-tuple-element.13.refs_0_), channel_id=1, source_target_pairs={{0,4},{4,8},{8,12},{12,0},{1,5},{5,9},{9,13},{13,1},{2,6},{6,10},{... | collective-permute-start | bytes 1572872 | tf_op jit(solution)/shard_map/ppermute | solution.py:249
  16.7 41.3 %collective-permute-start.3 = (bf16[2,128,2048]{2,1,0:T(8,128)(2,1)}, bf16[2,128,2048]{2,1,0:T(8,128)(2,1)S(1)}, u32[]{:S(2)}, u32[]{:S(2)}) collective-permute-start(bf16[2,128,2048]{2,1,0:T(8,128)(2,1)} %get-tuple-element.14.refs_3_.refs_0_), channel_id=1, source_target_pairs={{0,12},{4,0},{8,4},{12,8},{1,13},{5,1},{9,5},{13,9},{2,14},{6,2},{... | collective-permute-start | bytes 3145736 | tf_op jit(solution)/shard_map/ppermute | solution.py:249
  18.2 49.5 %collective-permute-start.4 = (bf16[2,128,1536]{2,1,0:T(8,128)(2,1)}, bf16[2,128,1536]{2,1,0:T(8,128)(2,1)S(1)}, u32[]{:S(2)}, u32[]{:S(2)}) collective-permute-start(bf16[2,128,1536]{2,1,0:T(8,128)(2,1)} %get-tuple-element.15.refs_6_.refs_0_), channel_id=1, source_target_pairs={{0,4},{4,8},{8,12},{12,0},{1,5},{5,9},{9,13},{13,1},{2,6},{6,10},{... | collective-permute-start | bytes 2359304 | tf_op jit(solution)/shard_map/ppermute | solution.py:249
  50.7 18.3 %collective-permute-start.5 = (bf16[2,128,1536]{2,1,0:T(8,128)(2,1)S(1)}, bf16[2,128,1536]{2,1,0:T(8,128)(2,1)S(1)}, u32[]{:S(2)}, u32[]{:S(2)}) collective-permute-start(bf16[2,128,1536]{2,1,0:T(8,128)(2,1)S(1)} %copy-done.14), channel_id=1, source_target_pairs={{0,12},{4,0},{8,4},{12,8},{1,13},{5,1},{9,5},{13,9},{2,14},{6,2},{... | collective-permute-start | bytes 2359304 | tf_op jit(solution)/shard_map/ppermute | solution.py:249
  52.0 50.9 %collective-permute-start.13 = (bf16[256,4608]{1,0:T(8,128)(2,1)}, bf16[256,4608]{1,0:T(8,128)(2,1)}, u32[]{:S(2)}, u32[]{:S(2)}) collective-permute-start(bf16[256,4608]{1,0:T(8,128)(2,1)} %refs_15_.1), channel_id=1, source_target_pairs={{0,18},{2,16},{16,2},{18,0},{1,19},{3,17},{17,3},{19,1},{4,22},{6,... | collective-permute-start | bytes 7077896 | tf_op jit(solution)/shard_map/ppermute | solution.py:249
  54.1 26.5 %collective-permute-start.18 = (bf16[2,256,1024]{2,1,0:T(8,128)(2,1)S(1)}, bf16[2,256,1024]{2,1,0:T(8,128)(2,1)S(1)}, u32[]{:S(2)}, u32[]{:S(2)}) collective-permute-start(bf16[2,256,1024]{2,1,0:T(8,128)(2,1)S(1)} %pad_maximum_fusion.1), channel_id=1, source_target_pairs={{0,1},{1,0},{2,3},{3,2},{4,5},{5,4},{6,7},{7,6},{8,9},{9,8},{10,11... | collective-permute-start | bytes 3145736 | tf_op jit(solution)/shard_map/ppermute | solution.py:249
  58.0 20.9 %collective-permute-start.8 = (bf16[128,2048]{1,0:T(8,128)(2,1)S(1)}, bf16[128,2048]{1,0:T(8,128)(2,1)S(1)}, u32[]{:S(2)}, u32[]{:S(2)}) collective-permute-start(bf16[128,2048]{1,0:T(8,128)(2,1)S(1)} %slice_bitcast_fusion.1), channel_id=1, source_target_pairs={{0,4},{4,8},{8,12},{12,0},{1,5},{5,9},{9,13},{13,1},{2,6},{6,10},{... | collective-permute-start | bytes 1572872 | tf_op jit(solution)/shard_map/ppermute | solution.py:249
  67.7 12.9 %collective-permute-start.9 = (bf16[128,2048]{1,0:T(8,128)(2,1)S(1)}, bf16[128,2048]{1,0:T(8,128)(2,1)S(1)}, u32[]{:S(2)}, u32[]{:S(2)}) collective-permute-start(bf16[128,2048]{1,0:T(8,128)(2,1)S(1)} %slice_bitcast_fusion), channel_id=1, source_target_pairs={{0,12},{4,0},{8,4},{12,8},{1,13},{5,1},{9,5},{13,9},{2,14},{6,2},{... | collective-permute-start | bytes 1572872 | tf_op jit(solution)/shard_map/ppermute | solution.py:249
  69.0 21.5 %collective-permute-start.1 = (bf16[2,128,1024]{2,1,0:T(8,128)(2,1)S(1)}, bf16[2,128,1024]{2,1,0:T(8,128)(2,1)S(1)}, u32[]{:S(2)}, u32[]{:S(2)}) collective-permute-start(bf16[2,128,1024]{2,1,0:T(8,128)(2,1)S(1)} %copy-done.15), channel_id=1, source_target_pairs={{0,12},{4,0},{8,4},{12,8},{1,13},{5,1},{9,5},{13,9},{2,14},{6,2},{... | collective-permute-start | bytes 1572872 | tf_op jit(solution)/shard_map/ppermute | solution.py:249
  78.9 58.7 %collective-permute-start.12 = (bf16[256,4608]{1,0:T(8,128)(2,1)}, bf16[256,4608]{1,0:T(8,128)(2,1)}, u32[]{:S(2)}, u32[]{:S(2)}) collective-permute-start(bf16[256,4608]{1,0:T(8,128)(2,1)} %refs_15_.1), channel_id=1, source_target_pairs={{0,1},{1,0},{2,3},{3,2},{4,5},{5,4},{6,7},{7,6},{8,9},{9,8},{10,11... | collective-permute-start | bytes 7077896 | tf_op jit(solution)/shard_map/ppermute | solution.py:249
  80.6 26.7 %collective-permute-start.10 = (bf16[128,1536]{1,0:T(8,128)(2,1)S(1)}, bf16[128,1536]{1,0:T(8,128)(2,1)S(1)}, u32[]{:S(2)}, u32[]{:S(2)}) collective-permute-start(bf16[128,1536]{1,0:T(8,128)(2,1)S(1)} %slice_bitcast_fusion.3), channel_id=1, source_target_pairs={{0,4},{4,8},{8,12},{12,0},{1,5},{5,9},{9,13},{13,1},{2,6},{6,10},{... | collective-permute-start | bytes 1179656 | tf_op jit(solution)/shard_map/ppermute | solution.py:249
  80.6 27.0 %collective-permute-start.11 = (bf16[128,1536]{1,0:T(8,128)(2,1)S(1)}, bf16[128,1536]{1,0:T(8,128)(2,1)S(1)}, u32[]{:S(2)}, u32[]{:S(2)}) collective-permute-start(bf16[128,1536]{1,0:T(8,128)(2,1)S(1)} %slice_bitcast_fusion.2), channel_id=1, source_target_pairs={{0,12},{4,0},{8,4},{12,8},{1,13},{5,1},{9,5},{13,9},{2,14},{6,2},{... | collective-permute-start | bytes 1179656 | tf_op jit(solution)/shard_map/ppermute | solution.py:249
  90.5 43.0 %collective-permute-start.23 = (bf16[4,2,256,512]{3,2,1,0:T(8,128)(2,1)}, bf16[4,2,256,512]{3,2,1,0:T(8,128)(2,1)}, u32[]{:S(2)}, u32[]{:S(2)}) collective-permute-start(bf16[4,2,256,512]{3,2,1,0:T(8,128)(2,1)} %get-tuple-element.19), channel_id=1, source_target_pairs={{0,1},{1,0},{2,3},{3,2},{4,5},{5,4},{6,7},{7,6},{8,9},{9,8},{10,11... | collective-permute-start | bytes 6291464 | tf_op jit(solution)/shard_map/ppermute | solution.py:249
  102.9 35.4 %collective-permute-start.14 = (bf16[256,4608]{1,0:T(8,128)(2,1)}, bf16[256,4608]{1,0:T(8,128)(2,1)}, u32[]{:S(2)}, u32[]{:S(2)}) collective-permute-start(bf16[256,4608]{1,0:T(8,128)(2,1)} %collective-permute-done.13.refs_15_), channel_id=1, source_target_pairs={{0,1},{1,0},{2,3},{3,2},{4,5},{5,4},{6,7},{7,6},{8,9},{9,8},{10,11... | collective-permute-start | bytes 7077896 | tf_op jit(solution)/shard_map/ppermute | solution.py:249
  117.0 11.9 %collective-permute-start.27 = (bf16[4,2,256,384]{3,2,1,0:T(8,128)(2,1)}, bf16[4,2,256,384]{3,2,1,0:T(8,128)(2,1)}, u32[]{:S(2)}, u32[]{:S(2)}) collective-permute-start(bf16[4,2,256,384]{3,2,1,0:T(8,128)(2,1)} %get-tuple-element.21), channel_id=1, source_target_pairs={{0,1},{1,0},{2,3},{3,2},{4,5},{5,4},{6,7},{7,6},{8,9},{9,8},{10,11... | collective-permute-start | bytes 4718600 | tf_op jit(solution)/shard_map/ppermute | solution.py:249
  127.3 23.5 %collective-permute-start.20 = (bf16[2,256,256]{2,1,0:T(8,128)(2,1)}, bf16[2,256,256]{2,1,0:T(8,128)(2,1)}, u32[]{:S(2)}, u32[]{:S(2)}) collective-permute-start(bf16[2,256,256]{2,1,0:T(8,128)(2,1)} %get-tuple-element.32), channel_id=1, source_target_pairs={{0,32},{32,64},{64,96},{96,0},{1,33},{33,65},{65,97},{97,1},{2,34}... | collective-permute-start | bytes 786440 | tf_op jit(solution)/shard_map/ppermute | solution.py:249
  128.9 22.5 %collective-permute-start.21 = (bf16[2,256,256]{2,1,0:T(8,128)(2,1)}, bf16[2,256,256]{2,1,0:T(8,128)(2,1)}, u32[]{:S(2)}, u32[]{:S(2)}) collective-permute-start(bf16[2,256,256]{2,1,0:T(8,128)(2,1)} %get-tuple-element.34), channel_id=1, source_target_pairs={{0,96},{32,0},{64,32},{96,64},{1,97},{33,1},{65,33},{97,65},{2,98}... | collective-permute-start | bytes 786440 | tf_op jit(solution)/shard_map/ppermute | solution.py:249
  133.6 17.9 %collective-permute-start.22 = (bf16[2,256,256]{2,1,0:T(8,128)(2,1)}, bf16[2,256,256]{2,1,0:T(8,128)(2,1)}, u32[]{:S(2)}, u32[]{:S(2)}) collective-permute-start(bf16[2,256,256]{2,1,0:T(8,128)(2,1)} %get-tuple-element.33), channel_id=1, source_target_pairs={{0,64},{32,96},{64,0},{96,32},{1,65},{33,97},{65,1},{97,33},{2,66}... | collective-permute-start | bytes 786440 | tf_op jit(solution)/shard_map/ppermute | solution.py:249
  137.6 16.5 %collective-permute-start.28 = (bf16[2,256,384]{2,1,0:T(8,128)(2,1)}, bf16[2,256,384]{2,1,0:T(8,128)(2,1)S(1)}, u32[]{:S(2)}, u32[]{:S(2)}) collective-permute-start(bf16[2,256,384]{2,1,0:T(8,128)(2,1)} %get-tuple-element.29), channel_id=1, source_target_pairs={{0,32},{32,64},{64,96},{96,0},{1,33},{33,65},{65,97},{97,1},{2,34}... | collective-permute-start | bytes 1179656 | tf_op jit(solution)/shard_map/ppermute | solution.py:249
  138.3 17.0 %collective-permute-start.29 = (bf16[2,256,384]{2,1,0:T(8,128)(2,1)}, bf16[2,256,384]{2,1,0:T(8,128)(2,1)S(1)}, u32[]{:S(2)}, u32[]{:S(2)}) collective-permute-start(bf16[2,256,384]{2,1,0:T(8,128)(2,1)} %get-tuple-element.31), channel_id=1, source_target_pairs={{0,96},{32,0},{64,32},{96,64},{1,97},{33,1},{65,33},{97,65},{2,98}... | collective-permute-start | bytes 1179656 | tf_op jit(solution)/shard_map/ppermute | solution.py:249
  150.8 16.6 %collective-permute-start.30 = (bf16[2,256,384]{2,1,0:T(8,128)(2,1)}, bf16[2,256,384]{2,1,0:T(8,128)(2,1)}, u32[]{:S(2)}, u32[]{:S(2)}) collective-permute-start(bf16[2,256,384]{2,1,0:T(8,128)(2,1)} %get-tuple-element.30), channel_id=1, source_target_pairs={{0,64},{32,96},{64,0},{96,32},{1,65},{33,97},{65,1},{97,33},{2,66}... | collective-permute-start | bytes 1179656 | tf_op jit(solution)/shard_map/ppermute | solution.py:249
  151.4 25.4 %collective-permute-start.24 = (bf16[2,256,512]{2,1,0:T(8,128)(2,1)}, bf16[2,256,512]{2,1,0:T(8,128)(2,1)}, u32[]{:S(2)}, u32[]{:S(2)}) collective-permute-start(bf16[2,256,512]{2,1,0:T(8,128)(2,1)} %get-tuple-element.26), channel_id=1, source_target_pairs={{0,32},{32,64},{64,96},{96,0},{1,33},{33,65},{65,97},{97,1},{2,34}... | collective-permute-start | bytes 1572872 | tf_op jit(solution)/shard_map/ppermute | solution.py:249
  151.5 25.3 %collective-permute-start.25 = (bf16[2,256,512]{2,1,0:T(8,128)(2,1)}, bf16[2,256,512]{2,1,0:T(8,128)(2,1)}, u32[]{:S(2)}, u32[]{:S(2)}) collective-permute-start(bf16[2,256,512]{2,1,0:T(8,128)(2,1)} %get-tuple-element.28), channel_id=1, source_target_pairs={{0,96},{32,0},{64,32},{96,64},{1,97},{33,1},{65,33},{97,65},{2,98}... | collective-permute-start | bytes 1572872 | tf_op jit(solution)/shard_map/ppermute | solution.py:249
  154.1 30.3 %collective-permute-start.26 = (bf16[2,256,512]{2,1,0:T(8,128)(2,1)}, bf16[2,256,512]{2,1,0:T(8,128)(2,1)}, u32[]{:S(2)}, u32[]{:S(2)}) collective-permute-start(bf16[2,256,512]{2,1,0:T(8,128)(2,1)} %get-tuple-element.27), channel_id=1, source_target_pairs={{0,64},{32,96},{64,0},{96,32},{1,65},{33,97},{65,1},{97,33},{2,66}... | collective-permute-start | bytes 1572872 | tf_op jit(solution)/shard_map/ppermute | solution.py:249
  155.4 31.6 %collective-permute-start.15 = (bf16[2,4,2,128,256]{4,3,2,1,0:T(8,128)(2,1)}, bf16[2,4,2,128,256]{4,3,2,1,0:T(8,128)(2,1)}, u32[]{:S(2)}, u32[]{:S(2)}) collective-permute-start(bf16[2,4,2,128,256]{4,3,2,1,0:T(8,128)(2,1)} %data_grad.3), channel_id=1, source_target_pairs={{0,2},{2,0},{1,3},{3,1},{4,6},{6,4},{5,7},{7,5},{8,10},{10,8},{9,1... | collective-permute-start | bytes 3145736 | tf_op jit(solution)/shard_map/ppermute | solution.py:249
  189.4 47.5 %collective-permute-start.16 = (bf16[2,4,2,128,256]{4,3,2,1,0:T(8,128)(2,1)}, bf16[2,4,2,128,256]{4,3,2,1,0:T(8,128)(2,1)S(1)}, u32[]{:S(2)}, u32[]{:S(2)}) collective-permute-start(bf16[2,4,2,128,256]{4,3,2,1,0:T(8,128)(2,1)} %pad_maximum_fusion), channel_id=1, source_target_pairs={{0,1},{1,0},{2,3},{3,2},{4,5},{5,4},{6,7},{7,6},{8,9},{9,8},{10,11... | collective-permute-start | bytes 3145736 | tf_op jit(solution)/shard_map/ppermute | solution.py:249
  192.7 40.0 %collective-permute-start.31 = (bf16[256,576]{1,0:T(8,128)(2,1)}, bf16[256,576]{1,0:T(8,128)(2,1)S(1)}, u32[]{:S(2)}, u32[]{:S(2)}) collective-permute-start(bf16[256,576]{1,0:T(8,128)(2,1)} %get-tuple-element.37), channel_id=1, source_target_pairs={{0,16},{16,0},{1,17},{17,1},{2,18},{18,2},{3,19},{19,3},{4,20},{20... | collective-permute-start | bytes 884744 | tf_op jit(solution)/shard_map/ppermute | solution.py:249
  192.7 40.0 %collective-permute-start.33 = (bf16[256,576]{1,0:T(8,128)(2,1)}, bf16[256,576]{1,0:T(8,128)(2,1)S(1)}, u32[]{:S(2)}, u32[]{:S(2)}) collective-permute-start(bf16[256,576]{1,0:T(8,128)(2,1)} %get-tuple-element.38), channel_id=1, source_target_pairs={{0,18},{2,16},{16,2},{18,0},{1,19},{3,17},{17,3},{19,1},{4,22},{6,... | collective-permute-start | bytes 884744 | tf_op jit(solution)/shard_map/ppermute | solution.py:249
  194.2 38.5 %collective-permute-start.32 = (bf16[256,576]{1,0:T(8,128)(2,1)}, bf16[256,576]{1,0:T(8,128)(2,1)}, u32[]{:S(2)}, u32[]{:S(2)}) collective-permute-start(bf16[256,576]{1,0:T(8,128)(2,1)} %slice_bitcast_fusion.5), channel_id=1, source_target_pairs={{0,2},{2,0},{1,3},{3,1},{4,6},{6,4},{5,7},{7,5},{8,10},{10,8},{9,1... | collective-permute-start | bytes 884744 | tf_op jit(solution)/shard_map/ppermute | solution.py:249
  196.7 13.5 %collective-permute-start.34 = (f32[1,4608]{1,0:T(1,128)S(1)}, f32[1,4608]{1,0:T(1,128)S(1)}, u32[]{:S(2)}, u32[]{:S(2)}) collective-permute-start(f32[1,4608]{1,0:T(1,128)S(1)} %copy-done.26), channel_id=1, source_target_pairs={{0,2},{2,0},{1,3},{3,1},{4,6},{6,4},{5,7},{7,5},{8,10},{10,8},{9,1... | collective-permute-start | bytes 55304 | tf_op jit(solution)/shard_map/ppermute | solution.py:249
  (37 other events, 599.9 us)

commit v3 on v2

--- a/solution.py
+++ b/solution.py
@@ -90,20 +90,28 @@
     )(projected, out_grad, gains)
 
 
-def turn_kernel(place, rows, out):
+def turn_kernel(place, rows, first, second):
     heads = rows.shape[-1]
     eye = (
         lax.broadcasted_iota(jnp.int32, (heads, heads), 0)
         == lax.broadcasted_iota(jnp.int32, (heads, heads), 1)
     ).astype(BF16)
     taken = [rows[m, near(place[0], j), 0] for j in range(4) for m in range(rows.shape[0])]
-    out[0] = nt(eye, jnp.concatenate(taken, axis=0)).astype(BF16)
+    part = nt(eye, jnp.concatenate(taken, axis=0)).astype(BF16)
+
+    @pl.when(pl.program_id(0) == 0)
+    def _():
+        first[...] = part
+
+    @pl.when(pl.program_id(0) == 1)
+    def _():
+        second[...] = part
 
 
 def turned(attention, place, across):
     micro, rows, heads = attention.shape
     each = rows // 16
-    shape = (2, heads, 4 * micro * each)
+    shape = (heads, 4 * micro * each)
     return pl.pallas_call(
         turn_kernel,
         grid_spec=pltpu.PrefetchScalarGridSpec(
@@ -115,11 +123,11 @@
                     lambda i, p: (0, 0, (p[1] ^ across) * 2 + (p[2] ^ i), 0, 0),
                 )
             ],
-            out_specs=pl.BlockSpec((1,) + shape[1:], lambda i, p: (i, 0, 0)),
+            out_specs=[pl.BlockSpec(shape, lambda i, p: (0, 0))] * 2,
         ),
-        out_shape=jax.ShapeDtypeStruct(shape, BF16),
+        out_shape=[jax.ShapeDtypeStruct(shape, BF16)] * 2,
         compiler_params=params(("arbitrary",)),
-        cost_estimate=cost(4 * heads * heads * shape[2], 8 * heads * shape[2]),
+        cost_estimate=cost(4 * heads * heads * shape[1], 8 * heads * shape[1]),
         name="turn",
     )(place, attention.reshape(micro, 4, 4, each, heads))
 
@@ -134,7 +142,7 @@
             take, refs = refs[:number], refs[number:]
             parts.append(jnp.concatenate([r[...].reshape(-1, r.shape[-1]) for r in take], axis=0))
         sides.append(parts[0] if len(parts) == 1 else jnp.concatenate(parts, axis=1))
-    weights, out = refs[:2], refs[2]
+    weights, outs = refs[:2], refs[2:]
 
     @pl.when(step == 0)
     def _():
@@ -150,7 +158,8 @@
 
     @pl.when(step == 3)
     def _():
-        out[...] = acc[...].astype(BF16).reshape(out.shape)
+        for h, out in enumerate(outs):
+            out[...] = acc[h].astype(BF16).reshape(out.shape)
 
 
 def data_grad(plan, weights):
@@ -164,7 +173,7 @@
             return pl.BlockSpec(a.shape[:2] + (size,), lambda t: (0, 0, t))
         return pl.BlockSpec((a.shape[0], size), lambda t: (0, t))
 
-    shape = (2, rows // 256, 2, 128, 256)
+    shape = (rows // 256, 2, 128, 256)
     flops = sum(
         2 * math.prod(a.shape) * 512 for _, arrays in plan for piece in arrays for a in piece
     )
@@ -172,8 +181,8 @@
         functools.partial(data_kernel, [(k, len(a[0])) for k, a in plan]),
         grid=(4,),
         in_specs=[rows_spec(a) for a in flat] + [pl.BlockSpec((256, width), lambda t: (0, t))] * 2,
-        out_specs=pl.BlockSpec(shape, lambda t: (0, 0, 0, 0, 0)),
-        out_shape=jax.ShapeDtypeStruct(shape, BF16),
+        out_specs=[pl.BlockSpec(shape, lambda t: (0, 0, 0, 0))] * 2,
+        out_shape=[jax.ShapeDtypeStruct(shape, BF16)] * 2,
         scratch_shapes=[pltpu.VMEM((2, rows, 256), F32)],
         compiler_params=params(("arbitrary",), 63),
         cost_estimate=cost(flops, 16 * 1024 * width),
@@ -191,7 +200,7 @@
         specs += [pl.BlockSpec((2, 128, zs * size), lambda i: (0, 0, i))] * 3
         specs += [pl.BlockSpec((128, zs * size), lambda i: (0, i))] * 2
     heads = [h for group in groups for h in group]
-    specs += [pl.BlockSpec((1, 256, 1024), lambda i, n=n: (n, 0, 0)) for _, n in heads]
+    specs += [pl.BlockSpec((256, 1024), lambda i: (0, 0))] * len(heads)
 
     def kernel(*refs):
         ins, outs = refs[: -len(groups)], refs[-len(groups) :]
@@ -201,7 +210,7 @@
                 [r[...].reshape(-1, zs * size) for r in ins[5 * k : 5 * k + 5]], axis=0
             )
             for h, block in enumerate(ins[5 * len(sizes) :]):
-                part = jnp.dot(block[0], rows, preferred_element_type=F32).astype(BF16)
+                part = jnp.dot(block[...], rows, preferred_element_type=F32).astype(BF16)
                 for n in range(zs):
                     outs[h // 2][n, h % 2, :, at : at + size] = part[:, n * size : (n + 1) * size]
             at += size
@@ -215,34 +224,32 @@
         compiler_params=params(("arbitrary",)),
         cost_estimate=cost(2 * len(heads) * 1024 * 1024 * total, 20 * 1024 * total),
         name="weight_sum",
-    )(*[a for piece in pieces for a in piece], *[h for h, _ in heads])
-
-
-def place_kernel(place, mine, over, mates, out):
+    )(*[a for piece in pieces for a in piece], *heads)
+
+
+def place_kernel(place, *refs):
+    out = refs[-1]
     for j in range(4):
-        for h, block in enumerate((mine.at[0], mates.at[0], over.at[0], mates.at[1])):
+        for h, block in enumerate(refs[:-1]):
             at = near(place[0], j) * 4 + (place[1] ^ (h // 2)) * 2 + (place[2] ^ (h % 2))
             out[:, pl.ds(at, 1)] = block[j][:, None]
 
 
 def placed(place, blocks):
-    mine, over, mates = blocks
-    shape = mine.shape[1:]
-    one = pl.BlockSpec((1,) + shape, lambda i, p: (0, 0, 0, 0, 0))
-    two = pl.BlockSpec((2,) + shape, lambda i, p: (0, 0, 0, 0, 0))
+    whole = pl.BlockSpec(blocks[0].shape, lambda i, p: (0, 0, 0, 0))
     return pl.pallas_call(
         place_kernel,
         grid_spec=pltpu.PrefetchScalarGridSpec(
             num_scalar_prefetch=1,
             grid=(1,),
-            in_specs=[one, one, two],
+            in_specs=[whole] * 4,
             out_specs=pl.BlockSpec((2, 16, 128, 256), lambda i, p: (0, 0, 0, 0)),
         ),
         out_shape=jax.ShapeDtypeStruct((2, 16, 128, 256), BF16),
         compiler_params=params(("arbitrary",)),
         cost_estimate=cost(1000000, 16 * 1024 * 1024 // 2),
         name="place",
-    )(place, mine, over, mates)
+    )(place, *blocks)
 
 
 def moved(value, axis, pairs):
@@ -265,9 +272,9 @@
         far.append((moved(a, X, ring(1)), moved(b, X, ring(-1))))
 
     def exchanged(mine, over):
-        over = moved(over, YH, swap())
-        mates = jnp.stack([mine[1], over[1]])
-        return mine, over, moved(mates, C, swap())
+        over, far_mate = [moved(v, YH, swap()) for v in over]
+        mate, far_mate = [moved(v, C, swap()) for v in (mine[1], far_mate)]
+        return mine[0], mate, over, far_mate
 
     over = turned(attention, place, 1)
     heads = exchanged(turned(attention, place, 0), over)
@@ -275,7 +282,7 @@
     over = moved(w_out, (YL, YH), swap(4))
     weights = (w_out, moved(w_out, C, swap()), over, moved(over, C, swap()))
 
-    for axis, bit in ((YH, 1), (YL, 1), (Z, 1), (Z, 2), (C, 1), (X, 1), (X, 2)):
+    for axis, bit in ((YH, 1), (YL, 1), (Z, 1), (Z, 2), (X, 1), (X, 2), (C, 1)):
         pairs = [(i, i ^ bit) for i in range(lax.axis_size(axis))]
         gain = gain + moved(gain, axis, pairs)
     new_gains = main_gains + factor * gain[0]
@@ -290,8 +297,7 @@
 
     def reduced(k):
         pieces = [(own[i], left[i], right[i], *far[i]) for i in SUMS[k]]
-        mine, over, mates = heads
-        keep, send = weight_sum(pieces, [((mine, 0), (over, 0)), ((mates, 0), (mates, 1))])
+        keep, send = weight_sum(pieces, (heads[0::2], heads[1::2]))
         other = moved(send, C, swap())
 
         def block(step):
@@ -307,10 +313,10 @@
     first, second = whole[:, :, : cols // 8], whole[:, :, cols // 8 :]
     ours, theirs = jnp.where(low == 0, first, second), jnp.where(low == 0, second, first)
     total = ours[0].astype(F32)
-    for value, axes, pairs in ((theirs[0], YL, swap()), (ours[1], YH, swap()), (theirs[1], (YL, YH), swap(4))):
+    for value, axes, pairs in ((ours[1], YH, swap()), (theirs[0], YL, swap()), (theirs[1], (YL, YH), swap(4))):
         got = moved(value, axes, pairs)
         total += got.astype(F32)
-    new_out = (main_out.T + factor * total.T).T
+    new_out = main_out + factor * total
     return (grad.reshape(attention.shape), new_out, new_gains)
 
 

time: 242 us -> 259 us (1.070)
  starting transfers between devices: 59.7 us -> 84.3 us
  waiting for transfers between devices: 99.9 us -> 96.3 us
  Pallas kernels: 51.1 us -> 47.6 us
    ppermute x41 -> x45, starting transfers between devices: 59.7 us -> 84.3 us  [moved(): return lax.ppermute(value, axis, pairs)]
    ppermute x41 -> x45, waiting for transfers between devices: 99.9 us -> 96.3 us  [moved(): return lax.ppermute(value, axis, pairs)]
  transfers between devices with their start and end apart: 41 -> 45, of which waited for: 14 -> 17; matrix products, arithmetic and copies ran while one was open for 9% -> 10% of each run, Pallas kernels for 19% -> 15%
where the time goes in v3:
time: 259 us; the launch traced here: 258 us
  waiting for transfers between devices  96.3 us (37%)
  starting transfers between devices  84.3 us (33%)
  Pallas kernels  47.6 us (18%)
  other arithmetic  17.1 us (7%)
  local copies, waits for them, and re-layouts  12.3 us (5%)
    ppermute x45, waiting for transfers between devices, moved(): return lax.ppermute(value, axis, pairs)  96.3 us
    ppermute x45, starting transfers between devices, moved(): return lax.ppermute(value, axis, pairs)  84.3 us
    pallas_call x2, Pallas kernels, data_grad(): pl.pallas_call(functools.partial(data_kernel, [(k, len(a[0])) for k, a in...  21 us
    pallas_call x3, Pallas kernels, weight_sum(): pl.pallas_call(kernel, grid=(4 // zs,), in_specs=specs, out_specs=[out] *...  15.5 us
    unnamed x56, local copies, waits for them, and re-layouts  7.55 us
    pallas_call x1, Pallas kernels, norm_pieces(): pl.pallas_call(functools.partial(norm_kernel, cols // 4), grid=(micro, ro...  6.12 us
    convert_element_type x3, other arithmetic, reduced(): blocks = [block(step).astype(BF16) for step in (1, -1, 2)]  5.73 us
  transfers between devices with their start and end apart: 45, of which 17 were waited for; matrix products, arithmetic and copies ran while one was open for 10% of the time, Pallas kernels for 15%

profile of v3, /device:TPU:1, one launch (start us, length us, event | category | flops | bytes accessed | tf_op | source)
XLA Modules:
  0.0 258.4 jit_solution(7976947319985899263)
XLA Ops:
  0.6 6.1 %norm_back.1 = (bf16[2,128,1024]{2,1,0:T(8,128)(2,1)}, bf16[2,128,2048]{2,1,0:T(8,128)(2,1)}, bf16[2,128,1536]{2,1,0:T(8,128)(2,1)}, f32[1,4608]{1,0:T(1,128)}) custom-call(bf16[2,128,4608]{2,1,0:T(8,128)(2,1)} %values.1, bf16[2,128,4608]{2,1,0:T(8,128)(2,1)} %upstream.1, f32[4608]{0:T(1024)} %gains.1), custom_call_target="tpu_custom_call" | custom-call | flops 18874368 | bytes 7077888 | tf_op jit(solution)/shard_map/norm_back/pallas_call | solution.py:78
  17.5 26.6 %collective-permute-done.refs_1_ = bf16[2,128,1024]{2,1,0:T(8,128)(2,1)} collective-permute-done((bf16[2,128,1024]{2,1,0:T(8,128)(2,1)}, bf16[2,128,1024]{2,1,0:T(8,128)(2,1)}, u32[]{:S(2)}, u32[]{:S(2)}) %collective-permute-start) | collective-permute-done | bytes 524320 | tf_op jit(solution)/shard_map/ppermute | solution.py:256
  46.6 3.0 %collective-permute-start.21 = (bf16[256,1024]{1,0:T(8,128)(2,1)S(1)}, bf16[256,1024]{1,0:T(8,128)(2,1)S(1)}, u32[]{:S(2)}, u32[]{:S(2)}) collective-permute-start(bf16[256,1024]{1,0:T(8,128)(2,1)S(1)} %get-tuple-element.31), channel_id=1, source_target_pairs={{0,2},{2,0},{1,3},{3,1},{4,6},{6,4},{5,7},{7,5},{8,10},{10,8},{9,1... | collective-permute-start | bytes 1572872 | tf_op jit(solution)/shard_map/ppermute | solution.py:256
  50.9 3.5 %collective-permute-start.20 = (bf16[256,1024]{1,0:T(8,128)(2,1)S(1)}, bf16[256,1024]{1,0:T(8,128)(2,1)S(1)}, u32[]{:S(2)}, u32[]{:S(2)}) collective-permute-start(bf16[256,1024]{1,0:T(8,128)(2,1)S(1)} %get-tuple-element.30), channel_id=1, source_target_pairs={{0,1},{1,0},{2,3},{3,2},{4,5},{5,4},{6,7},{7,6},{8,9},{9,8},{10,11... | collective-permute-start | bytes 1572872 | tf_op jit(solution)/shard_map/ppermute | solution.py:256
  54.4 4.3 %collective-permute-done.21 = bf16[256,1024]{1,0:T(8,128)(2,1)S(1)} collective-permute-done((bf16[256,1024]{1,0:T(8,128)(2,1)S(1)}, bf16[256,1024]{1,0:T(8,128)(2,1)S(1)}, u32[]{:S(2)}, u32[]{:S(2)}) %collective-permute-start.21) | collective-permute-done | bytes 524320 | tf_op jit(solution)/shard_map/ppermute | solution.py:256
  58.8 2.7 %collective-permute-start.14 = (bf16[256,4608]{1,0:T(8,128)(2,1)S(1)}, bf16[256,4608]{1,0:T(8,128)(2,1)}, u32[]{:S(2)}, u32[]{:S(2)}) collective-permute-start(bf16[256,4608]{1,0:T(8,128)(2,1)S(1)} %copy-done.26), channel_id=1, source_target_pairs={{0,18},{2,16},{16,2},{18,0},{1,19},{3,17},{17,3},{19,1},{4,22},{6,... | collective-permute-start | bytes 7077896 | tf_op jit(solution)/shard_map/ppermute | solution.py:256
  61.5 8.5 %collective-permute-done.19.refs_6_ = bf16[256,1024]{1,0:T(8,128)(2,1)S(1)} collective-permute-done((bf16[256,1024]{1,0:T(8,128)(2,1)S(1)}, bf16[256,1024]{1,0:T(8,128)(2,1)S(1)}, u32[]{:S(2)}, u32[]{:S(2)}) %collective-permute-start.19) | collective-permute-done | bytes 524320 | tf_op jit(solution)/shard_map/ppermute | solution.py:256
  70.0 3.9 %collective-permute-start.22 = (bf16[256,1024]{1,0:T(8,128)(2,1)S(1)}, bf16[256,1024]{1,0:T(8,128)(2,1)S(1)}, u32[]{:S(2)}, u32[]{:S(2)}) collective-permute-start(bf16[256,1024]{1,0:T(8,128)(2,1)S(1)} %collective-permute-done.21), channel_id=1, source_target_pairs={{0,1},{1,0},{2,3},{3,2},{4,5},{5,4},{6,7},{7,6},{8,9},{9,8},{10,11... | collective-permute-start | bytes 1572872 | tf_op jit(solution)/shard_map/ppermute | solution.py:256
  74.1 2.5 collective-permute-start.9
  76.8 2.7 %collective-permute-start.7 = (bf16[128,1024]{1,0:T(8,128)(2,1)S(1)}, bf16[128,1024]{1,0:T(8,128)(2,1)S(1)}, u32[]{:S(2)}, u32[]{:S(2)}) collective-permute-start(bf16[128,1024]{1,0:T(8,128)(2,1)S(1)} %slice_bitcast_fusion.8), channel_id=1, source_target_pairs={{0,12},{4,0},{8,4},{12,8},{1,13},{5,1},{9,5},{13,9},{2,14},{6,2},{... | collective-permute-start | bytes 786440 | tf_op jit(solution)/shard_map/ppermute | solution.py:256
  79.4 9.2 %collective-permute-done.8.refs_11_.refs_3_ = bf16[128,2048]{1,0:T(8,128)(2,1)S(1)} collective-permute-done((bf16[128,2048]{1,0:T(8,128)(2,1)S(1)}, bf16[128,2048]{1,0:T(8,128)(2,1)S(1)}, u32[]{:S(2)}, u32[]{:S(2)}) %collective-permute-start.8) | collective-permute-done | bytes 524320 | tf_op jit(solution)/shard_map/ppermute | solution.py:256
  88.6 2.7 %collective-permute-start.11 = (bf16[128,1536]{1,0:T(8,128)(2,1)S(1)}, bf16[128,1536]{1,0:T(8,128)(2,1)S(1)}, u32[]{:S(2)}, u32[]{:S(2)}) collective-permute-start(bf16[128,1536]{1,0:T(8,128)(2,1)S(1)} %slice_bitcast_fusion.2), channel_id=1, source_target_pairs={{0,12},{4,0},{8,4},{12,8},{1,13},{5,1},{9,5},{13,9},{2,14},{6,2},{... | collective-permute-start | bytes 1179656 | tf_op jit(solution)/shard_map/ppermute | solution.py:256
  92.5 6.2 %weight_sum.4 = (bf16[4,2,256,512]{3,2,1,0:T(8,128)(2,1)S(1)}, bf16[4,2,256,512]{3,2,1,0:T(8,128)(2,1)}) custom-call(bf16[2,128,2048]{2,1,0:T(8,128)(2,1)S(1)} %copy-done.10, bf16[2,128,2048]{2,1,0:T(8,128)(2,1)S(1)} %collective-permute-done.2.refs_4_.refs_1_, bf16[2,128,2048]{2,1,0:T(8,128)(2,1)S(1)} %copy-done.6, ...), custom_call_target="tpu_custom_call" | custom-call | flops 4294967296 | bytes 10485760 | tf_op jit(solution)/shard_map/weight_sum/pallas_call | solution.py:218
  98.8 3.9 %collective-permute-done.10.refs_13_.refs_3_ = bf16[128,1536]{1,0:T(8,128)(2,1)S(1)} collective-permute-done((bf16[128,1536]{1,0:T(8,128)(2,1)S(1)}, bf16[128,1536]{1,0:T(8,128)(2,1)S(1)}, u32[]{:S(2)}, u32[]{:S(2)}) %collective-permute-start.10) | collective-permute-done | bytes 393248 | tf_op jit(solution)/shard_map/ppermute | solution.py:256
  103.5 4.8 %weight_sum.5 = (bf16[4,2,256,384]{3,2,1,0:T(8,128)(2,1)S(1)}, bf16[4,2,256,384]{3,2,1,0:T(8,128)(2,1)}) custom-call(bf16[2,128,1536]{2,1,0:T(8,128)(2,1)S(1)} %copy-done.11, bf16[2,128,1536]{2,1,0:T(8,128)(2,1)S(1)} %copy-done.8, bf16[2,128,1536]{2,1,0:T(8,128)(2,1)S(1)} %collective-permute-done.5.refs_8_.refs_2_, ...), custom_call_target="tpu_custom_call" | custom-call | flops 3221225472 | bytes 7864320 | tf_op jit(solution)/shard_map/weight_sum/pallas_call | solution.py:218
  109.6 4.5 %weight_sum.3 = (bf16[4,2,256,256]{3,2,1,0:T(8,128)(2,1)S(1)}, bf16[4,2,256,256]{3,2,1,0:T(8,128)(2,1)}) custom-call(bf16[2,128,1024]{2,1,0:T(8,128)(2,1)S(1)} %copy-done.12, bf16[2,128,1024]{2,1,0:T(8,128)(2,1)} %collective-permute-done.refs_1_, bf16[2,128,1024]{2,1,0:T(8,128)(2,1)} %collective-permute-done.1.refs_2_, ...), custom_call_target="tpu_custom_call" | custom-call | flops 2147483648 | bytes 5242880 | tf_op jit(solution)/shard_map/weight_sum/pallas_call | solution.py:218
  114.7 9.3 %collective-permute-done.14.refs_15_ = bf16[256,4608]{1,0:T(8,128)(2,1)} collective-permute-done((bf16[256,4608]{1,0:T(8,128)(2,1)S(1)}, bf16[256,4608]{1,0:T(8,128)(2,1)}, u32[]{:S(2)}, u32[]{:S(2)}) %collective-permute-start.14) | collective-permute-done | bytes 2359328 | tf_op jit(solution)/shard_map/ppermute | solution.py:256
  127.6 2.9 %collective-permute-start.38 = (f32[1,4608]{1,0:T(1,128)S(1)}, f32[1,4608]{1,0:T(1,128)S(1)}, u32[]{:S(2)}, u32[]{:S(2)}) collective-permute-start(f32[1,4608]{1,0:T(1,128)S(1)} %copy-done.24), channel_id=1, source_target_pairs={{0,2},{2,0},{1,3},{3,1},{4,6},{6,4},{5,7},{7,5},{8,10},{10,8},{9,1... | collective-permute-start | bytes 55304 | tf_op jit(solution)/shard_map/ppermute | solution.py:256
  137.6 3.1 %collective-permute-start.41 = (f32[1,4608]{1,0:T(1,128)S(1)}, f32[1,4608]{1,0:T(1,128)S(1)}, u32[]{:S(2)}, u32[]{:S(2)}) collective-permute-start(f32[1,4608]{1,0:T(1,128)S(1)} %add.225), channel_id=1, source_target_pairs={{0,64},{32,96},{64,0},{96,32},{1,65},{33,97},{65,1},{97,33},{2,66}... | collective-permute-start | bytes 55304 | tf_op jit(solution)/shard_map/ppermute | solution.py:256
  142.3 2.7 %collective-permute-done.42 = f32[1,4608]{1,0:T(1,128)S(1)} collective-permute-done((f32[1,4608]{1,0:T(1,128)S(1)}, f32[1,4608]{1,0:T(1,128)S(1)}, u32[]{:S(2)}, u32[]{:S(2)}) %collective-permute-start.42) | collective-permute-done | bytes 18464 | tf_op jit(solution)/shard_map/ppermute | solution.py:256
  145.7 3.6 %collective-permute-done.43 = f32[1,4608]{1,0:T(1,128)S(1)} collective-permute-done((f32[1,4608]{1,0:T(1,128)S(1)}, f32[1,4608]{1,0:T(1,128)S(1)}, u32[]{:S(2)}, u32[]{:S(2)}) %collective-permute-start.43) | collective-permute-done | bytes 18464 | tf_op jit(solution)/shard_map/ppermute | solution.py:256
  151.9 7.6 %collective-permute-start.12 = (bf16[256,4608]{1,0:T(8,128)(2,1)}, bf16[256,4608]{1,0:T(8,128)(2,1)}, u32[]{:S(2)}, u32[]{:S(2)}) collective-permute-start(bf16[256,4608]{1,0:T(8,128)(2,1)} %refs_15_.1), channel_id=1, source_target_pairs={{0,1},{1,0},{2,3},{3,2},{4,5},{5,4},{6,7},{7,6},{8,9},{9,8},{10,11... | collective-permute-start | bytes 7077896 | tf_op jit(solution)/shard_map/ppermute | solution.py:256
  164.3 2.8 %fusion.6 = (bf16[2,256,512]{2,1,0:T(8,128)(2,1)}, bf16[2,256,512]{2,1,0:T(8,128)(2,1)}, bf16[2,256,512]{2,1,0:T(8,128)(2,1)}) fusion(bf16[4,2,256,512]{3,2,1,0:T(8,128)(2,1)} %collective-permute-done.27, s32[]{:T(128)S(6)} %select_n.49, bf16[4,2,256,512]{3,2,1,0:T(8,128)(2,1)S(1)} %get-tuple-element.34, s32[]{:T(128)S(6)} %select_n.51, s32[]{:T(128)S(6)} %select_n.50), kind=kLoop, calls=%fused_computation.19 | loop fusion | flops 3145728 | bytes 4718604 | tf_op jit(solution)/shard_map/convert_element_type | solution.py:308
  167.1 5.9 %collective-permute-done.32 = bf16[2,256,384]{2,1,0:T(8,128)(2,1)S(1)} collective-permute-done((bf16[2,256,384]{2,1,0:T(8,128)(2,1)S(1)}, bf16[2,256,384]{2,1,0:T(8,128)(2,1)S(1)}, u32[]{:S(2)}, u32[]{:S(2)}) %collective-permute-start.32) | collective-permute-done | bytes 393248 | tf_op jit(solution)/shard_map/ppermute | solution.py:256
  173.0 2.7 %collective-permute-start.29 = (bf16[2,256,512]{2,1,0:T(8,128)(2,1)}, bf16[2,256,512]{2,1,0:T(8,128)(2,1)}, u32[]{:S(2)}, u32[]{:S(2)}) collective-permute-start(bf16[2,256,512]{2,1,0:T(8,128)(2,1)} %get-tuple-element.44), channel_id=1, source_target_pairs={{0,96},{32,0},{64,32},{96,64},{1,97},{33,1},{65,33},{97,65},{2,98}... | collective-permute-start | bytes 1572872 | tf_op jit(solution)/shard_map/ppermute | solution.py:256
  177.5 3.8 %collective-permute-start.30 = (bf16[2,256,512]{2,1,0:T(8,128)(2,1)}, bf16[2,256,512]{2,1,0:T(8,128)(2,1)}, u32[]{:S(2)}, u32[]{:S(2)}) collective-permute-start(bf16[2,256,512]{2,1,0:T(8,128)(2,1)} %get-tuple-element.43), channel_id=1, source_target_pairs={{0,64},{32,96},{64,0},{96,32},{1,65},{33,97},{65,1},{97,33},{2,66}... | collective-permute-start | bytes 1572872 | tf_op jit(solution)/shard_map/ppermute | solution.py:256
  185.7 6.5 %collective-permute-done.28 = bf16[2,256,512]{2,1,0:T(8,128)(2,1)} collective-permute-done((bf16[2,256,512]{2,1,0:T(8,128)(2,1)}, bf16[2,256,512]{2,1,0:T(8,128)(2,1)}, u32[]{:S(2)}, u32[]{:S(2)}) %collective-permute-start.28) | collective-permute-done | bytes 524320 | tf_op jit(solution)/shard_map/ppermute | solution.py:256
  192.1 13.5 %collective-permute-start.44 = (f32[1,4608]{1,0:T(1,128)}, f32[1,4608]{1,0:T(1,128)S(1)}, u32[]{:S(2)}, u32[]{:S(2)}) collective-permute-start(f32[1,4608]{1,0:T(1,128)} %add.228), channel_id=1, source_target_pairs={{0,1},{1,0},{2,3},{3,2},{4,5},{5,4},{6,7},{7,6},{8,9},{9,8},{10,11... | collective-permute-start | bytes 55304 | tf_op jit(solution)/shard_map/ppermute | solution.py:256
  212.9 10.5 %data_grad.3 = (bf16[4,2,128,256]{3,2,1,0:T(8,128)(2,1)}, bf16[4,2,128,256]{3,2,1,0:T(8,128)(2,1)}) custom-call(bf16[2,128,1024]{2,1,0:T(8,128)(2,1)} %get-tuple-element.21.refs_0_, bf16[2,128,1024]{2,1,0:T(8,128)(2,1)} %collective-permute-done.refs_1_, bf16[2,128,1024]{2,1,0:T(8,128)(2,1)} %collective-permute-done.1.refs_2_, ...), custom_call_target="tpu_custom_call" | custom-call | flops 4831838208 | bytes 18874368 | tf_op jit(solution)/shard_map/data_grad/pallas_call | solution.py:180
  228.2 10.5 %data_grad.2 = (bf16[4,2,128,256]{3,2,1,0:T(8,128)(2,1)}, bf16[4,2,128,256]{3,2,1,0:T(8,128)(2,1)}) custom-call(bf16[2,128,1024]{2,1,0:T(8,128)(2,1)} %get-tuple-element.21.refs_0_, bf16[2,128,1024]{2,1,0:T(8,128)(2,1)} %collective-permute-done.refs_1_, bf16[2,128,1024]{2,1,0:T(8,128)(2,1)} %collective-permute-done.1.refs_2_, ...), custom_call_target="tpu_custom_call" | custom-call | flops 4831838208 | bytes 18874368 | tf_op jit(solution)/shard_map/data_grad/pallas_call | solution.py:180
  245.3 2.2 fusion.5
  249.6 6.8 %collective-permute-done.16.refs_2_ = bf16[4,2,128,256]{3,2,1,0:T(8,128)(2,1)S(1)} collective-permute-done((bf16[4,2,128,256]{3,2,1,0:T(8,128)(2,1)}, bf16[4,2,128,256]{3,2,1,0:T(8,128)(2,1)S(1)}, u32[]{:S(2)}, u32[]{:S(2)}) %collective-permute-start.16) | collective-permute-done | bytes 524320 | tf_op jit(solution)/shard_map/ppermute | solution.py:256
  (148 shorter events, 68.0 us)
Async XLA Ops:
  6.7 43.9 %collective-permute-start.2 = (bf16[2,128,2048]{2,1,0:T(8,128)(2,1)}, bf16[2,128,2048]{2,1,0:T(8,128)(2,1)S(1)}, u32[]{:S(2)}, u32[]{:S(2)}) collective-permute-start(bf16[2,128,2048]{2,1,0:T(8,128)(2,1)} %get-tuple-element.22.refs_3_.refs_0_), channel_id=1, source_target_pairs={{0,4},{4,8},{8,12},{12,0},{1,5},{5,9},{9,13},{13,1},{2,6},{6,10},{... | collective-permute-start | bytes 3145736 | tf_op jit(solution)/shard_map/ppermute | solution.py:256
  8.8 35.3 %collective-permute-start = (bf16[2,128,1024]{2,1,0:T(8,128)(2,1)}, bf16[2,128,1024]{2,1,0:T(8,128)(2,1)}, u32[]{:S(2)}, u32[]{:S(2)}) collective-permute-start(bf16[2,128,1024]{2,1,0:T(8,128)(2,1)} %get-tuple-element.21.refs_0_), channel_id=1, source_target_pairs={{0,4},{4,8},{8,12},{12,0},{1,5},{5,9},{9,13},{13,1},{2,6},{6,10},{... | collective-permute-start | bytes 1572872 | tf_op jit(solution)/shard_map/ppermute | solution.py:256
  10.0 36.6 %collective-permute-start.1 = (bf16[2,128,1024]{2,1,0:T(8,128)(2,1)}, bf16[2,128,1024]{2,1,0:T(8,128)(2,1)}, u32[]{:S(2)}, u32[]{:S(2)}) collective-permute-start(bf16[2,128,1024]{2,1,0:T(8,128)(2,1)} %get-tuple-element.21.refs_0_), channel_id=1, source_target_pairs={{0,12},{4,0},{8,4},{12,8},{1,13},{5,1},{9,5},{13,9},{2,14},{6,2},{... | collective-permute-start | bytes 1572872 | tf_op jit(solution)/shard_map/ppermute | solution.py:256
  11.5 39.4 %collective-permute-start.3 = (bf16[2,128,2048]{2,1,0:T(8,128)(2,1)}, bf16[2,128,2048]{2,1,0:T(8,128)(2,1)S(1)}, u32[]{:S(2)}, u32[]{:S(2)}) collective-permute-start(bf16[2,128,2048]{2,1,0:T(8,128)(2,1)} %get-tuple-element.22.refs_3_.refs_0_), channel_id=1, source_target_pairs={{0,12},{4,0},{8,4},{12,8},{1,13},{5,1},{9,5},{13,9},{2,14},{6,2},{... | collective-permute-start | bytes 3145736 | tf_op jit(solution)/shard_map/ppermute | solution.py:256
  11.6 62.3 %collective-permute-start.4 = (bf16[2,128,1536]{2,1,0:T(8,128)(2,1)}, bf16[2,128,1536]{2,1,0:T(8,128)(2,1)S(1)}, u32[]{:S(2)}, u32[]{:S(2)}) collective-permute-start(bf16[2,128,1536]{2,1,0:T(8,128)(2,1)} %get-tuple-element.23.refs_6_.refs_0_), channel_id=1, source_target_pairs={{0,4},{4,8},{8,12},{12,0},{1,5},{5,9},{9,13},{13,1},{2,6},{6,10},{... | collective-permute-start | bytes 2359304 | tf_op jit(solution)/shard_map/ppermute | solution.py:256
  44.1 30.0 %collective-permute-start.5 = (bf16[2,128,1536]{2,1,0:T(8,128)(2,1)S(1)}, bf16[2,128,1536]{2,1,0:T(8,128)(2,1)S(1)}, u32[]{:S(2)}, u32[]{:S(2)}) collective-permute-start(bf16[2,128,1536]{2,1,0:T(8,128)(2,1)S(1)} %copy-done.11), channel_id=1, source_target_pairs={{0,12},{4,0},{8,4},{12,8},{1,13},{5,1},{9,5},{13,9},{2,14},{6,2},{... | collective-permute-start | bytes 2359304 | tf_op jit(solution)/shard_map/ppermute | solution.py:256
  46.6 12.1 %collective-permute-start.21 = (bf16[256,1024]{1,0:T(8,128)(2,1)S(1)}, bf16[256,1024]{1,0:T(8,128)(2,1)S(1)}, u32[]{:S(2)}, u32[]{:S(2)}) collective-permute-start(bf16[256,1024]{1,0:T(8,128)(2,1)S(1)} %get-tuple-element.31), channel_id=1, source_target_pairs={{0,2},{2,0},{1,3},{3,1},{4,6},{6,4},{5,7},{7,5},{8,10},{10,8},{9,1... | collective-permute-start | bytes 1572872 | tf_op jit(solution)/shard_map/ppermute | solution.py:256
  50.6 19.4 %collective-permute-start.19 = (bf16[256,1024]{1,0:T(8,128)(2,1)S(1)}, bf16[256,1024]{1,0:T(8,128)(2,1)S(1)}, u32[]{:S(2)}, u32[]{:S(2)}) collective-permute-start(bf16[256,1024]{1,0:T(8,128)(2,1)S(1)} %get-tuple-element.29), channel_id=1, source_target_pairs={{0,2},{2,0},{1,3},{3,1},{4,6},{6,4},{5,7},{7,5},{8,10},{10,8},{9,1... | collective-permute-start | bytes 1572872 | tf_op jit(solution)/shard_map/ppermute | solution.py:256
  50.9 25.8 %collective-permute-start.20 = (bf16[256,1024]{1,0:T(8,128)(2,1)S(1)}, bf16[256,1024]{1,0:T(8,128)(2,1)S(1)}, u32[]{:S(2)}, u32[]{:S(2)}) collective-permute-start(bf16[256,1024]{1,0:T(8,128)(2,1)S(1)} %get-tuple-element.30), channel_id=1, source_target_pairs={{0,1},{1,0},{2,3},{3,2},{4,5},{5,4},{6,7},{7,6},{8,9},{9,8},{10,11... | collective-permute-start | bytes 1572872 | tf_op jit(solution)/shard_map/ppermute | solution.py:256
  58.8 65.2 %collective-permute-start.14 = (bf16[256,4608]{1,0:T(8,128)(2,1)S(1)}, bf16[256,4608]{1,0:T(8,128)(2,1)}, u32[]{:S(2)}, u32[]{:S(2)}) collective-permute-start(bf16[256,4608]{1,0:T(8,128)(2,1)S(1)} %copy-done.26), channel_id=1, source_target_pairs={{0,18},{2,16},{16,2},{18,0},{1,19},{3,17},{17,3},{19,1},{4,22},{6,... | collective-permute-start | bytes 7077896 | tf_op jit(solution)/shard_map/ppermute | solution.py:256
  73.9 14.7 %collective-permute-start.8 = (bf16[128,2048]{1,0:T(8,128)(2,1)S(1)}, bf16[128,2048]{1,0:T(8,128)(2,1)S(1)}, u32[]{:S(2)}, u32[]{:S(2)}) collective-permute-start(bf16[128,2048]{1,0:T(8,128)(2,1)S(1)} %slice_bitcast_fusion.1), channel_id=1, source_target_pairs={{0,4},{4,8},{8,12},{12,0},{1,5},{5,9},{9,13},{13,1},{2,6},{6,10},{... | collective-permute-start | bytes 1572872 | tf_op jit(solution)/shard_map/ppermute | solution.py:256
  74.1 14.6 %collective-permute-start.9 = (bf16[128,2048]{1,0:T(8,128)(2,1)S(1)}, bf16[128,2048]{1,0:T(8,128)(2,1)S(1)}, u32[]{:S(2)}, u32[]{:S(2)}) collective-permute-start(bf16[128,2048]{1,0:T(8,128)(2,1)S(1)} %slice_bitcast_fusion), channel_id=1, source_target_pairs={{0,12},{4,0},{8,4},{12,8},{1,13},{5,1},{9,5},{13,9},{2,14},{6,2},{... | collective-permute-start | bytes 1572872 | tf_op jit(solution)/shard_map/ppermute | solution.py:256
  76.7 32.9 %collective-permute-start.6 = (bf16[128,1024]{1,0:T(8,128)(2,1)S(1)}, bf16[128,1024]{1,0:T(8,128)(2,1)S(1)}, u32[]{:S(2)}, u32[]{:S(2)}) collective-permute-start(bf16[128,1024]{1,0:T(8,128)(2,1)S(1)} %slice_bitcast_fusion.9), channel_id=1, source_target_pairs={{0,4},{4,8},{8,12},{12,0},{1,5},{5,9},{9,13},{13,1},{2,6},{6,10},{... | collective-permute-start | bytes 786440 | tf_op jit(solution)/shard_map/ppermute | solution.py:256
  76.8 32.8 %collective-permute-start.7 = (bf16[128,1024]{1,0:T(8,128)(2,1)S(1)}, bf16[128,1024]{1,0:T(8,128)(2,1)S(1)}, u32[]{:S(2)}, u32[]{:S(2)}) collective-permute-start(bf16[128,1024]{1,0:T(8,128)(2,1)S(1)} %slice_bitcast_fusion.8), channel_id=1, source_target_pairs={{0,12},{4,0},{8,4},{12,8},{1,13},{5,1},{9,5},{13,9},{2,14},{6,2},{... | collective-permute-start | bytes 786440 | tf_op jit(solution)/shard_map/ppermute | solution.py:256
  88.6 14.0 %collective-permute-start.10 = (bf16[128,1536]{1,0:T(8,128)(2,1)S(1)}, bf16[128,1536]{1,0:T(8,128)(2,1)S(1)}, u32[]{:S(2)}, u32[]{:S(2)}) collective-permute-start(bf16[128,1536]{1,0:T(8,128)(2,1)S(1)} %slice_bitcast_fusion.3), channel_id=1, source_target_pairs={{0,4},{4,8},{8,12},{12,0},{1,5},{5,9},{9,13},{13,1},{2,6},{6,10},{... | collective-permute-start | bytes 1179656 | tf_op jit(solution)/shard_map/ppermute | solution.py:256
  88.6 14.9 %collective-permute-start.11 = (bf16[128,1536]{1,0:T(8,128)(2,1)S(1)}, bf16[128,1536]{1,0:T(8,128)(2,1)S(1)}, u32[]{:S(2)}, u32[]{:S(2)}) collective-permute-start(bf16[128,1536]{1,0:T(8,128)(2,1)S(1)} %slice_bitcast_fusion.2), channel_id=1, source_target_pairs={{0,12},{4,0},{8,4},{12,8},{1,13},{5,1},{9,5},{13,9},{2,14},{6,2},{... | collective-permute-start | bytes 1179656 | tf_op jit(solution)/shard_map/ppermute | solution.py:256
  102.7 61.2 %collective-permute-start.27 = (bf16[4,2,256,512]{3,2,1,0:T(8,128)(2,1)}, bf16[4,2,256,512]{3,2,1,0:T(8,128)(2,1)}, u32[]{:S(2)}, u32[]{:S(2)}) collective-permute-start(bf16[4,2,256,512]{3,2,1,0:T(8,128)(2,1)} %get-tuple-element.35), channel_id=1, source_target_pairs={{0,1},{1,0},{2,3},{3,2},{4,5},{5,4},{6,7},{7,6},{8,9},{9,8},{10,11... | collective-permute-start | bytes 6291464 | tf_op jit(solution)/shard_map/ppermute | solution.py:256
  109.5 42.3 %collective-permute-start.31 = (bf16[4,2,256,384]{3,2,1,0:T(8,128)(2,1)}, bf16[4,2,256,384]{3,2,1,0:T(8,128)(2,1)}, u32[]{:S(2)}, u32[]{:S(2)}) collective-permute-start(bf16[4,2,256,384]{3,2,1,0:T(8,128)(2,1)} %get-tuple-element.37), channel_id=1, source_target_pairs={{0,1},{1,0},{2,3},{3,2},{4,5},{5,4},{6,7},{7,6},{8,9},{9,8},{10,11... | collective-permute-start | bytes 4718600 | tf_op jit(solution)/shard_map/ppermute | solution.py:256
  124.0 89.0 %collective-permute-start.15 = (bf16[256,4608]{1,0:T(8,128)(2,1)}, bf16[256,4608]{1,0:T(8,128)(2,1)}, u32[]{:S(2)}, u32[]{:S(2)}) collective-permute-start(bf16[256,4608]{1,0:T(8,128)(2,1)} %collective-permute-done.14.refs_15_), channel_id=1, source_target_pairs={{0,1},{1,0},{2,3},{3,2},{4,5},{5,4},{6,7},{7,6},{8,9},{9,8},{10,11... | collective-permute-start | bytes 7077896 | tf_op jit(solution)/shard_map/ppermute | solution.py:256
  125.9 24.9 %collective-permute-start.24 = (bf16[2,256,256]{2,1,0:T(8,128)(2,1)S(1)}, bf16[2,256,256]{2,1,0:T(8,128)(2,1)S(1)}, u32[]{:S(2)}, u32[]{:S(2)}) collective-permute-start(bf16[2,256,256]{2,1,0:T(8,128)(2,1)S(1)} %get-tuple-element.48), channel_id=1, source_target_pairs={{0,32},{32,64},{64,96},{96,0},{1,33},{33,65},{65,97},{97,1},{2,34}... | collective-permute-start | bytes 786440 | tf_op jit(solution)/shard_map/ppermute | solution.py:256
  151.9 74.2 %collective-permute-start.12 = (bf16[256,4608]{1,0:T(8,128)(2,1)}, bf16[256,4608]{1,0:T(8,128)(2,1)}, u32[]{:S(2)}, u32[]{:S(2)}) collective-permute-start(bf16[256,4608]{1,0:T(8,128)(2,1)} %refs_15_.1), channel_id=1, source_target_pairs={{0,1},{1,0},{2,3},{3,2},{4,5},{5,4},{6,7},{7,6},{8,9},{9,8},{10,11... | collective-permute-start | bytes 7077896 | tf_op jit(solution)/shard_map/ppermute | solution.py:256
  163.8 13.7 %collective-permute-start.34 = (bf16[2,256,384]{2,1,0:T(8,128)(2,1)S(1)}, bf16[2,256,384]{2,1,0:T(8,128)(2,1)}, u32[]{:S(2)}, u32[]{:S(2)}) collective-permute-start(bf16[2,256,384]{2,1,0:T(8,128)(2,1)S(1)} %get-tuple-element.46), channel_id=1, source_target_pairs={{0,64},{32,96},{64,0},{96,32},{1,65},{33,97},{65,1},{97,33},{2,66}... | collective-permute-start | bytes 1179656 | tf_op jit(solution)/shard_map/ppermute | solution.py:256
  173.0 19.2 %collective-permute-start.28 = (bf16[2,256,512]{2,1,0:T(8,128)(2,1)}, bf16[2,256,512]{2,1,0:T(8,128)(2,1)}, u32[]{:S(2)}, u32[]{:S(2)}) collective-permute-start(bf16[2,256,512]{2,1,0:T(8,128)(2,1)} %get-tuple-element.42), channel_id=1, source_target_pairs={{0,32},{32,64},{64,96},{96,0},{1,33},{33,65},{65,97},{97,1},{2,34}... | collective-permute-start | bytes 1572872 | tf_op jit(solution)/shard_map/ppermute | solution.py:256
  173.0 32.7 %collective-permute-start.29 = (bf16[2,256,512]{2,1,0:T(8,128)(2,1)}, bf16[2,256,512]{2,1,0:T(8,128)(2,1)}, u32[]{:S(2)}, u32[]{:S(2)}) collective-permute-start(bf16[2,256,512]{2,1,0:T(8,128)(2,1)} %get-tuple-element.44), channel_id=1, source_target_pairs={{0,96},{32,0},{64,32},{96,64},{1,97},{33,1},{65,33},{97,65},{2,98}... | collective-permute-start | bytes 1572872 | tf_op jit(solution)/shard_map/ppermute | solution.py:256
  177.5 28.2 %collective-permute-start.30 = (bf16[2,256,512]{2,1,0:T(8,128)(2,1)}, bf16[2,256,512]{2,1,0:T(8,128)(2,1)}, u32[]{:S(2)}, u32[]{:S(2)}) collective-permute-start(bf16[2,256,512]{2,1,0:T(8,128)(2,1)} %get-tuple-element.43), channel_id=1, source_target_pairs={{0,64},{32,96},{64,0},{96,32},{1,65},{33,97},{65,1},{97,33},{2,66}... | collective-permute-start | bytes 1572872 | tf_op jit(solution)/shard_map/ppermute | solution.py:256
  192.1 46.6 %collective-permute-start.44 = (f32[1,4608]{1,0:T(1,128)}, f32[1,4608]{1,0:T(1,128)S(1)}, u32[]{:S(2)}, u32[]{:S(2)}) collective-permute-start(f32[1,4608]{1,0:T(1,128)} %add.228), channel_id=1, source_target_pairs={{0,1},{1,0},{2,3},{3,2},{4,5},{5,4},{6,7},{7,6},{8,9},{9,8},{10,11... | collective-permute-start | bytes 55304 | tf_op jit(solution)/shard_map/ppermute | solution.py:256
  209.8 30.1 %collective-permute-start.36 = (bf16[256,576]{1,0:T(8,128)(2,1)}, bf16[256,576]{1,0:T(8,128)(2,1)S(1)}, u32[]{:S(2)}, u32[]{:S(2)}) collective-permute-start(bf16[256,576]{1,0:T(8,128)(2,1)} %get-tuple-element.53), channel_id=1, source_target_pairs={{0,16},{16,0},{1,17},{17,1},{2,18},{18,2},{3,19},{19,3},{4,20},{20... | collective-permute-start | bytes 884744 | tf_op jit(solution)/shard_map/ppermute | solution.py:256
  211.0 32.6 %collective-permute-start.37 = (bf16[256,576]{1,0:T(8,128)(2,1)}, bf16[256,576]{1,0:T(8,128)(2,1)S(1)}, u32[]{:S(2)}, u32[]{:S(2)}) collective-permute-start(bf16[256,576]{1,0:T(8,128)(2,1)} %get-tuple-element.54), channel_id=1, source_target_pairs={{0,18},{2,16},{16,2},{18,0},{1,19},{3,17},{17,3},{19,1},{4,22},{6,... | collective-permute-start | bytes 884744 | tf_op jit(solution)/shard_map/ppermute | solution.py:256
  223.5 17.0 %collective-permute-start.17 = (bf16[4,2,128,256]{3,2,1,0:T(8,128)(2,1)}, bf16[4,2,128,256]{3,2,1,0:T(8,128)(2,1)}, u32[]{:S(2)}, u32[]{:S(2)}) collective-permute-start(bf16[4,2,128,256]{3,2,1,0:T(8,128)(2,1)} %get-tuple-element.27), channel_id=1, source_target_pairs={{0,2},{2,0},{1,3},{3,1},{4,6},{6,4},{5,7},{7,5},{8,10},{10,8},{9,1... | collective-permute-start | bytes 1572872 | tf_op jit(solution)/shard_map/ppermute | solution.py:256
  226.1 19.2 %collective-permute-start.35 = (bf16[256,576]{1,0:T(8,128)(2,1)}, bf16[256,576]{1,0:T(8,128)(2,1)}, u32[]{:S(2)}, u32[]{:S(2)}) collective-permute-start(bf16[256,576]{1,0:T(8,128)(2,1)} %slice_bitcast_fusion.6), channel_id=1, source_target_pairs={{0,2},{2,0},{1,3},{3,1},{4,6},{6,4},{5,7},{7,5},{8,10},{10,8},{9,1... | collective-permute-start | bytes 884744 | tf_op jit(solution)/shard_map/ppermute | solution.py:256
  239.9 16.5 %collective-permute-start.16 = (bf16[4,2,128,256]{3,2,1,0:T(8,128)(2,1)}, bf16[4,2,128,256]{3,2,1,0:T(8,128)(2,1)S(1)}, u32[]{:S(2)}, u32[]{:S(2)}) collective-permute-start(bf16[4,2,128,256]{3,2,1,0:T(8,128)(2,1)} %get-tuple-element.26), channel_id=1, source_target_pairs={{0,2},{2,0},{1,3},{3,1},{4,6},{6,4},{5,7},{7,5},{8,10},{10,8},{9,1... | collective-permute-start | bytes 1572872 | tf_op jit(solution)/shard_map/ppermute | solution.py:256
  240.5 15.9 %collective-permute-start.18 = (bf16[4,2,128,256]{3,2,1,0:T(8,128)(2,1)}, bf16[4,2,128,256]{3,2,1,0:T(8,128)(2,1)S(1)}, u32[]{:S(2)}, u32[]{:S(2)}) collective-permute-start(bf16[4,2,128,256]{3,2,1,0:T(8,128)(2,1)} %collective-permute-done.17), channel_id=1, source_target_pairs={{0,1},{1,0},{2,3},{3,2},{4,5},{5,4},{6,7},{7,6},{8,9},{9,8},{10,11... | collective-permute-start | bytes 1572872 | tf_op jit(solution)/shard_map/ppermute | solution.py:256
  (40 other events, 526.5 us)
